TPU v7x, 128 devices: a whole 4x4x4 slice. The times are simulated.
128 devices in a mesh: rep: 1, r: 4 (over x), s: 32 (over y, z, core).
Axes of the slice: x: 4, y: 4, z: 4, core: 2. Of those that a mesh axis runs over, the one named last changes fastest.
Arguments:
- x: bfloat16 [128, 2048, 1152], P(('rep', 'r', 's'))
- dy: bfloat16 [128, 2048, 1152], P(('rep', 'r', 's'))
- w_gate: bfloat16 [2, 1152, 4608], P(None, 's')
- w_up: bfloat16 [2, 1152, 4608], P(None, 's')
- w_down: bfloat16 [2, 4608, 1152], P(None, 's')
- m_w_gate: float32 [2, 1152, 4608], P(None, 's')
- m_w_up: float32 [2, 1152, 4608], P(None, 's')
- m_w_down: float32 [2, 4608, 1152], P(None, 's')
- v_w_gate: float32 [2, 1152, 4608], P(None, 's')
- v_w_up: float32 [2, 1152, 4608], P(None, 's')
- v_w_down: float32 [2, 4608, 1152], P(None, 's')
Outputs:
- output 1: bfloat16 [2, 1152, 4608], P('rep', 's')
- output 2: bfloat16 [2, 1152, 4608], P('rep', 's')
- output 3: bfloat16 [2, 4608, 1152], P('rep', 's')
- output 4: float32 [2, 1152, 4608], P('rep', 's')
- output 5: float32 [2, 1152, 4608], P('rep', 's')
- output 6: float32 [2, 4608, 1152], P('rep', 's')
- output 7: float32 [2, 1152, 4608], P('rep', 's')
- output 8: float32 [2, 1152, 4608], P('rep', 's')
- output 9: float32 [2, 4608, 1152], P('rep', 's')
All inputs are finite; a program needn't handle non-finite values.
Results may differ from a plain program's by a relative error of at most 0.022.
Values are sent between devices in bfloat16 or wider.
A program may use at most 1.5 GiB of HBM per device.

v0:
```python
import jax
import jax.numpy as jnp
from jax import lax
from jax.sharding import PartitionSpec as P

NAMES = ("w_gate", "w_up", "w_down")


def matmul(a, w):
    return jnp.dot(a, w, preferred_element_type=jnp.float32).astype(jnp.bfloat16)


def normed(h):
    wide = h.astype(jnp.float32)
    scale = lax.rsqrt(jnp.mean(wide**2, -1, keepdims=True) + 1e-6)
    return (wide * scale).astype(jnp.bfloat16)


def layer(h, w):
    a = normed(h)
    gate = jnp.dot(a, w["w_gate"], preferred_element_type=jnp.float32)
    up = jnp.dot(a, w["w_up"], preferred_element_type=jnp.float32)
    return h + matmul((jax.nn.silu(gate) * up).astype(jnp.bfloat16), w["w_down"])


def adamw(w, m, v, g):
    m = 0.9 * m + 0.1 * g
    v = 0.95 * v + 0.05 * g * g
    step = m * lax.rsqrt(v + 1e-8) + 0.1 * w
    return (w - 0.02 * step).astype(jnp.bfloat16), m, v


def clipped(gradients, sum_of_squares, count):
    factor = jnp.minimum(1.0, 0.5 * lax.rsqrt(sum_of_squares / count + 1e-30))
    return [g * factor for g in gradients]


def solution(mesh):
    def fetched(weights, number):
        return {name: lax.all_gather(w[number], "s", axis=0, tiled=True) for name, w in zip(NAMES, weights, strict=True)}

    def summed(term):
        return lax.psum(lax.psum_scatter(term, "s", scatter_dimension=0, tiled=True), "r")

    def step(x, dy, *arrays):
        weights, m, v = (arrays[i : i + 3] for i in (0, 3, 6))
        layers = weights[0].shape[0]
        h, kept = x[0], []
        for number in range(layers):
            kept.append(h)
            h = layer(h, fetched(weights, number))
        by_h, mine = dy[0], [None] * layers
        for number in reversed(range(layers)):
            _, back = jax.vjp(lambda w, h: layer(h, w), fetched(weights, number), kept[number])
            by_w, by_h = back(by_h)
            mine[number] = [summed(by_w[name]) for name in NAMES]
        gradients = [jnp.stack([mine[number][i] for number in range(layers)]).astype(jnp.float32) for i in range(3)]
        squares = lax.psum(sum(jnp.sum(g * g) for g in gradients), "s")
        gradients = clipped(gradients, squares, lax.psum(1, "s") * sum(g.size for g in gradients))
        new = [adamw(w.astype(jnp.float32), m, v, g) for w, m, v, g in zip(weights, m, v, gradients, strict=True)]
        return tuple(one[which] for which in range(3) for one in new)

    states, cut = P(("rep", "r", "s"), None, None), P(None, "s", None)
    return jax.shard_map(
        step,
        mesh=mesh,
        in_specs=(states, states) + (cut,) * 9,
        out_specs=(P("rep", "s", None),) * 9,
        check_vma=False,
    )
```

profile of v0, /device:TPU:0, one launch (start us, length us, event | category | flops | bytes accessed | tf_op | source)
XLA Modules:
  0.0 1450.6 jit_solution(7361994888032664887)
XLA Ops:
  35.4 61.1 %all-gather.13.cloned.1.call-done = bf16[1,1152,4608]{2,0,1:T(2,128)(2,1)} async-done(((bf16[1,36,4608]{2,0,1:T(2,128)(2,1)}), bf16[1,1152,4608]{2,0,1:T(2,128)(2,1)}) %all-gather.13.cloned.1.call-update) | async-done | bytes 10616848 | tf_op jit(solution)/shard_map/all_gather | solution.py:40
  96.5 34.5 %fusion.33 = f32[2048,4608]{1,0:T(8,128)} fusion(bf16[1,1152,4608]{2,0,1:T(2,128)(2,1)} %all-gather.13.cloned.1.call-done, bf16[1,2048,1152]{1,2,0:T(8,128)(2,1)} %copy.54, f32[2048]{0:T(1024)S(1)} %add_rsqrt_fusion), kind=kOutput, calls=%fused_computation.48 | convolution fusion | flops 21750349824 | bytes 53092352 | tf_op jit(solution)/shard_map/dot_general | solution.py:21
  131.1 50.6 %all-gather.15.cloned.1.call-done = bf16[1,1152,4608]{2,0,1:T(2,128)(2,1)} async-done(((bf16[1,36,4608]{2,0,1:T(2,128)(2,1)}), bf16[1,1152,4608]{2,0,1:T(2,128)(2,1)}) %all-gather.15.cloned.1.call-update) | async-done | bytes 10616848 | tf_op jit(solution)/shard_map/all_gather | solution.py:40
  181.7 49.3 %multiply_convert_fusion.1 = (bf16[2048,4608]{1,0:T(8,128)(2,1)}, f32[2048,4608]{1,0:T(8,128)}) fusion(f32[2048,4608]{1,0:T(8,128)} %fusion.33, bf16[1,1152,4608]{2,0,1:T(2,128)(2,1)} %all-gather.15.cloned.1.call-done, bf16[1,2048,1152]{1,2,0:T(8,128)(2,1)} %copy.54, f32[2048]{0:T(1024)S(1)} %add_rsqrt_fusion), kind=kOutput, calls=%fused_computation.17 | convolution fusion | flops 21806972928 | bytes 109715456 | tf_op jit(solution)/shard_map/dot_general | solution.py:22
  241.8 30.5 %fusion.44 = (f32[2048]{0:T(1024)S(1)}, bf16[2048,1152]{0,1:T(8,128)(2,1)}) fusion(bf16[2048,4608]{1,0:T(8,128)(2,1)} %get-tuple-element.65, bf16[1,4608,1152]{2,1,0:T(8,128)(2,1)} %all-gather.17.cloned.1.call-done, bf16[1,2048,1152]{1,2,0:T(8,128)(2,1)} %copy.54), kind=kOutput, calls=%fused_computation.59 | convolution fusion | flops 21755066368 | bytes 38936576 | tf_op jit(solution)/shard_map/dot_general | solution.py:10
  272.3 29.6 %all-gather.21.cloned.1.call-done = bf16[1,4608,1152]{2,1,0:T(8,128)(2,1)} async-done(((bf16[1,144,1152]{2,1,0:T(8,128)(2,1)}), bf16[1,4608,1152]{2,1,0:T(8,128)(2,1)}) %all-gather.21.cloned.1.call-update) | async-done | bytes 10616848 | tf_op jit(solution)/shard_map/all_gather | solution.py:40
  301.8 31.5 %convolution_convert_fusion.1 = bf16[2048,4608]{1,0:T(8,128)(2,1)} fusion(bf16[1,4608,1152]{2,1,0:T(8,128)(2,1)} %all-gather.21.cloned.1.call-done, bf16[1,2048,1152]{2,1,0:T(8,128)(2,1)} %param.12), kind=kOutput, calls=%fused_computation.26 | convolution fusion | flops 21752709120 | bytes 34209792 | tf_op jit(solution)/shard_map/transpose(jvp())/dot_general | solution.py:10
  333.3 53.6 %all-gather.23.cloned.1.call-done = bf16[1,1152,4608]{2,0,1:T(2,128)(2,1)} async-done(((bf16[1,36,4608]{2,0,1:T(2,128)(2,1)}), bf16[1,1152,4608]{2,0,1:T(2,128)(2,1)}) %all-gather.23.cloned.1.call-update) | async-done | bytes 10616848 | tf_op jit(solution)/shard_map/all_gather | solution.py:40
  387.0 34.6 %fusion.23 = f32[2048,4608]{1,0:T(8,128)} fusion(bf16[1,1152,4608]{2,0,1:T(2,128)(2,1)} %all-gather.23.cloned.1.call-done, bf16[2048,1152]{0,1:T(8,128)(2,1)} %get-tuple-element.68, f32[2048]{0:T(1024)S(1)} %fusion.99), kind=kOutput, calls=%fused_computation.38 | convolution fusion | flops 21750349824 | bytes 53092352 | tf_op jit(solution)/shard_map/jvp()/dot_general | solution.py:22
  421.6 50.4 %all-gather.19.cloned.1.call-done = bf16[1,1152,4608]{2,0,1:T(2,128)(2,1)} async-done(((bf16[1,36,4608]{2,0,1:T(2,128)(2,1)}), bf16[1,1152,4608]{2,0,1:T(2,128)(2,1)}) %all-gather.19.cloned.1.call-update) | async-done | bytes 10616848 | tf_op jit(solution)/shard_map/all_gather | solution.py:40
  472.0 57.2 %fusion.6 = (bf16[2048,4608]{1,0:T(8,128)(2,1)}, f32[2048,4608]{1,0:T(8,128)}) fusion(f32[2048,4608]{1,0:T(8,128)} %fusion.23, bf16[2048,4608]{1,0:T(8,128)(2,1)} %convolution_convert_fusion.1, bf16[1,1152,4608]{2,0,1:T(2,128)(2,1)} %all-gather.19.cloned.1.call-done, bf16[2048,1152]{0,1:T(8,128)(2,1)} %get-tuple-element.68, f32[2048]{0:T(1024)S(1)} %fusion.99), kind=kOutput, calls=%fused_computation.8 | convolution fusion | flops 21863596032 | bytes 128589824 | tf_op jit(solution)/shard_map/jvp()/dot_general | solution.py:21
  529.2 34.3 %fusion.50 = bf16[2048,1152]{0,1:T(8,128)(2,1)} fusion(bf16[2048,4608]{1,0:T(8,128)(2,1)} %get-tuple-element.69, bf16[1,1152,4608]{2,0,1:T(2,128)(2,1)} %all-gather.19.cloned.1.call-done), kind=kOutput, calls=%fused_computation.63 | convolution fusion | flops 21743271936 | bytes 34209792 | tf_op jit(solution)/shard_map/transpose(jvp())/dot_general | solution.py:21
  563.5 41.1 %fusion.46 = (f32[2048]{0:T(1024)S(1)}, bf16[2048,1152]{0,1:T(8,128)(2,1)}) fusion(bf16[2048,1152]{0,1:T(8,128)(2,1)} %get-tuple-element.68, bf16[2048,1152]{0,1:T(8,128)(2,1)} %fusion.50, bf16[1,1152,4608]{2,0,1:T(2,128)(2,1)} %all-gather.23.cloned.1.call-done, bf16[2048,4608]{1,0:T(8,128)(2,1)} %convolution_convert_fusion.1, ...), kind=kOutput, calls=%fused_computation.61 | convolution fusion | flops 21814048768 | bytes 81403904 | tf_op jit(solution)/shard_map/transpose(jvp())/dot_general | solution.py:22
  615.4 29.7 %convolution_convert_fusion.3 = bf16[4608,1152]{1,0:T(8,128)(2,1)} fusion(bf16[2048,4608]{1,0:T(8,128)(2,1)} %get-tuple-element.65, bf16[2048,1152]{0,1:T(8,128)(2,1)S(1)} %fusion.63), kind=kOutput, calls=%fused_computation.28 | convolution fusion | flops 21748580352 | bytes 34209792 | tf_op jit(solution)/shard_map/transpose(jvp())/dot_general | solution.py:10
  645.1 31.8 %convolution_convert_fusion = bf16[2048,4608]{1,0:T(8,128)(2,1)} fusion(bf16[2048,1152]{0,1:T(8,128)(2,1)} %copy-done.3, bf16[1,4608,1152]{2,1,0:T(8,128)(2,1)} %all-gather.17.cloned.1.call-done), kind=kOutput, calls=%fused_computation.25 | convolution fusion | flops 21752709120 | bytes 34209792 | tf_op jit(solution)/shard_map/transpose(jvp())/dot_general | solution.py:10
  676.9 42.7 %fusion.18 = bf16[1152,4608]{1,0:T(8,128)(2,1)} fusion(f32[2048,4608]{1,0:T(8,128)} %fusion.33, f32[2048,4608]{1,0:T(8,128)} %get-tuple-element.66, bf16[2048,4608]{1,0:T(8,128)(2,1)} %convolution_convert_fusion, bf16[1,2048,1152]{1,2,0:T(8,128)(2,1)} %copy.54, f32[2048]{0:T(1024)S(1)} %copy-done.24), kind=kOutput, calls=%fused_computation.23 | convolution fusion | flops 21859467264 | bytes 109715456 | tf_op jit(solution)/shard_map/transpose(jvp())/dot_general | solution.py:21
  719.6 27.2 %convolution_convert_fusion.4 = bf16[1152,4608]{1,0:T(8,128)(2,1)} fusion(bf16[2048,4608]{1,0:T(8,128)(2,1)} %get-tuple-element.69, bf16[2048,1152]{0,1:T(8,128)(2,1)S(1)} %copy-done.2, f32[2048]{0:T(1024)S(1)} %copy-done.19), kind=kOutput, calls=%fused_computation.29 | convolution fusion | flops 21750349824 | bytes 34217984 | tf_op jit(solution)/shard_map/transpose(jvp())/dot_general | solution.py:21
  746.8 34.5 %fusion.21 = bf16[1152,4608]{1,0:T(8,128)(2,1)} fusion(bf16[2048,4608]{1,0:T(8,128)(2,1)} %convolution_convert_fusion, f32[2048,4608]{1,0:T(8,128)} %fusion.33, bf16[1,2048,1152]{1,2,0:T(8,128)(2,1)} %copy.54, f32[2048]{0:T(1024)S(1)} %copy-done.24), kind=kOutput, calls=%fused_computation.24 | convolution fusion | flops 21812281344 | bytes 71966720 | tf_op jit(solution)/shard_map/transpose(jvp())/dot_general | solution.py:22
  781.3 37.3 %convolution_convert_fusion.2 = bf16[4608,1152]{1,0:T(8,128)(2,1)} fusion(f32[2048,4608]{1,0:T(8,128)} %fusion.23, bf16[1,2048,1152]{2,1,0:T(8,128)(2,1)} %param.12, f32[2048,4608]{1,0:T(8,128)} %get-tuple-element.70), kind=kOutput, calls=%fused_computation.27 | convolution fusion | flops 21805203456 | bytes 90832896 | tf_op jit(solution)/shard_map/transpose(jvp())/dot_general | solution.py:10
  819.4 34.6 %fusion.17 = bf16[1152,4608]{1,0:T(8,128)(2,1)} fusion(bf16[2048,4608]{1,0:T(8,128)(2,1)} %convolution_convert_fusion.1, bf16[2048,1152]{0,1:T(8,128)(2,1)} %get-tuple-element.68, f32[2048]{0:T(1024)S(1)} %copy-done.20, f32[2048,4608]{1,0:T(8,128)} %get-tuple-element.70), kind=kOutput, calls=%fused_computation.22 | convolution fusion | flops 21812281344 | bytes 71966720 | tf_op jit(solution)/shard_map/transpose(jvp())/dot_general | solution.py:22
  854.0 290.3 %fusion.105 = (bf16[40,4608]{1,0:T(8,128)(2,1)S(1)}, bf16[40,4608]{1,0:T(8,128)(2,1)}, bf16[40,4608]{1,0:T(8,128)(2,1)S(1)}, bf16[40,4608]{1,0:T(8,128)(2,1)S(1)}) fusion(bf16[1152,4608]{1,0:T(8,128)(2,1)} %convolution_convert_fusion.4, bf16[1152,4608]{1,0:T(8,128)(2,1)} %fusion.18, bf16[1152,4608]{1,0:T(8,128)(2,1)} %fusion.17, bf16[1152,4608]{1,0:T(8,128)(2,1)} %fusion.21), kind=kCustom, calls=%all-reduce-scatter.4 | all-reduce-scatter fusion | flops 23592960 | bytes 43942400
  1228.5 17.3 %concatenate.3 = bf16[164,4608]{1,0:T(8,128)(2,1)} concatenate(bf16[4,4608]{1,0:T(4,128)(2,1)S(1)} %collective-permute-done.15, bf16[40,4608]{1,0:T(8,128)(2,1)} %copy-done.16, bf16[40,4608]{1,0:T(8,128)(2,1)} %copy-done.15, bf16[40,4608]{1,0:T(8,128)(2,1)} %copy-done.14, bf16[40,4608]{1,0:T(8,128)(2,1)} %copy-done.5), dimensions={0} | concatenate | bytes 3022848
  1286.3 63.7 %all-reduce.12.cloned.1.call-done = (bf16[1,36,4608]{2,1,0:T(8,128)(2,1)}, bf16[1,36,4608]{2,1,0:T(8,128)(2,1)}, bf16[1,36,4608]{2,1,0:T(8,128)(2,1)}, bf16[1,36...) async-done(((bf16[1,36,4608]{2,1,0:T(8,128)(2,1)}, bf16[1,36,4608]{2,1,0:T(8,128)(2,1)}, bf16[1,36,4608]{2,1,0:T(8,128)(2,1)}, ...) | async-done | bytes 1990672 | tf_op jit(solution)/shard_map/psum | solution.py:43
  1358.1 67.7 %psum.55 = f32[]{:T(128)} all-reduce(f32[]{:T(128)S(6)} %add.111), channel_id=1, replica_groups=mesh['rep'=1,'r'=4,'s'=32] {'s'}, use_global_device_ids=true, to_apply=%region_18.19 | all-reduce | flops 1 | bytes 8 | tf_op jit(solution)/shard_map/psum | solution.py:58
  (138 shorter events, 197.5 us)
Async XLA Ops:
  7.2 89.3 %all-gather.13.cloned.1.call-start = ((), (), s32[]{:S(2)}) async-start(), calls=%async_computation.4 | async-start | bytes 21897216 | tf_op jit(solution)/shard_map/all_gather | solution.py:40
  10.9 170.8 %all-gather.15.cloned.1.call-start = ((), (), s32[]{:S(2)}) async-start(), calls=%async_computation.5 | async-start | bytes 21897216 | tf_op jit(solution)/shard_map/all_gather | solution.py:40
  14.5 227.2 %all-gather.17.cloned.1.call-start = ((), (), s32[]{:S(2)}) async-start(), calls=%async_computation.6 | async-start | bytes 10948608 | tf_op jit(solution)/shard_map/all_gather | solution.py:40
  16.6 285.3 %all-gather.21.cloned.1.call-start = ((), (), s32[]{:S(2)}) async-start(), calls=%async_computation.8 | async-start | bytes 10948608 | tf_op jit(solution)/shard_map/all_gather | solution.py:40
  17.1 369.8 %all-gather.23.cloned.1.call-start = ((), (), s32[]{:S(2)}) async-start(), calls=%async_computation.9 | async-start | bytes 21897216 | tf_op jit(solution)/shard_map/all_gather | solution.py:40
  17.7 454.3 %all-gather.19.cloned.1.call-start = ((), (), s32[]{:S(2)}) async-start(), calls=%async_computation.7 | async-start | bytes 21897216 | tf_op jit(solution)/shard_map/all_gather | solution.py:40
  18.3 1267.9 %reduce-scatter.11.cloned.1.call-start = ((), (), s32[]{:S(2)}) async-start(), calls=%async_computation.2 | async-start | bytes 10948608 | tf_op jit(solution)/shard_map/reduce_scatter | solution.py:43
  645.1 641.2 %reduce-scatter.13.cloned.1.call-start = ((), (), s32[]{:S(2)}) async-start(), calls=%async_computation.3 | async-start | bytes 10948608 | tf_op jit(solution)/shard_map/reduce_scatter | solution.py:43
  818.7 531.2 %all-reduce.12.cloned.1.call-start = ((), (), s32[]{:S(2)}) async-start(), calls=%async_computation.10 | async-start | bytes 4276224 | tf_op jit(solution)/shard_map/psum | solution.py:43
  1144.3 23.9 %collective-permute-start.10 = (bf16[40,4608]{1,0:T(8,128)(2,1)S(1)}, bf16[40,4608]{1,0:T(8,128)(2,1)S(1)}, u32[]{:S(2)}, u32[]{:S(2)}) collective-permute-start(bf16[40,4608]{1,0:T(8,128)(2,1)S(1)} %get-tuple-element.49), channel_id=1, source_target_pairs={{0,3},{1,4},{2,5},{3,6},{4,7},{5,8},{6,9},{7,10},{8,11},{9,12},{10... | collective-permute-start | bytes 1105928
  1145.6 29.9 %collective-permute-start.8 = (bf16[40,4608]{1,0:T(8,128)(2,1)S(1)}, bf16[40,4608]{1,0:T(8,128)(2,1)S(1)}, u32[]{:S(2)}, u32[]{:S(2)}) collective-permute-start(bf16[40,4608]{1,0:T(8,128)(2,1)S(1)} %get-tuple-element.49), channel_id=1, source_target_pairs={{0,1},{1,2},{2,3},{3,4},{4,5},{5,6},{6,7},{7,8},{8,9},{9,10},{10,1... | collective-permute-start | bytes 1105928
  1147.1 15.3 %collective-permute-start.11 = (bf16[4,4608]{1,0:T(4,128)(2,1)S(1)}, bf16[4,4608]{1,0:T(4,128)(2,1)S(1)}, u32[]{:S(2)}, u32[]{:S(2)}) collective-permute-start(bf16[4,4608]{1,0:T(4,128)(2,1)S(1)} %slice.29), channel_id=1, source_target_pairs={{0,4},{1,5},{2,6},{3,7},{4,8},{5,9},{6,10},{7,11},{8,12},{9,13},{1... | collective-permute-start | bytes 110600
  1153.5 10.2 collective-permute-start.15
  1162.4 15.7 %collective-permute-start.9 = (bf16[40,4608]{1,0:T(8,128)(2,1)S(1)}, bf16[40,4608]{1,0:T(8,128)(2,1)S(1)}, u32[]{:S(2)}, u32[]{:S(2)}) collective-permute-start(bf16[40,4608]{1,0:T(8,128)(2,1)S(1)} %get-tuple-element.49), channel_id=1, source_target_pairs={{0,2},{1,3},{2,4},{3,5},{4,6},{5,7},{6,8},{7,9},{8,10},{9,11},{10,... | collective-permute-start | bytes 1105928
  1163.8 16.7 %collective-permute-start.12 = (bf16[40,4608]{1,0:T(8,128)(2,1)S(1)}, bf16[40,4608]{1,0:T(8,128)(2,1)S(1)}, u32[]{:S(2)}, u32[]{:S(2)}) collective-permute-start(bf16[40,4608]{1,0:T(8,128)(2,1)S(1)} %get-tuple-element.48), channel_id=1, source_target_pairs={{0,1},{1,2},{2,3},{3,4},{4,5},{5,6},{6,7},{7,8},{8,9},{9,10},{10,1... | collective-permute-start | bytes 1105928
  1165.8 16.7 %collective-permute-start.13 = (bf16[40,4608]{1,0:T(8,128)(2,1)S(1)}, bf16[40,4608]{1,0:T(8,128)(2,1)S(1)}, u32[]{:S(2)}, u32[]{:S(2)}) collective-permute-start(bf16[40,4608]{1,0:T(8,128)(2,1)S(1)} %get-tuple-element.48), channel_id=1, source_target_pairs={{0,2},{1,3},{2,4},{3,5},{4,6},{5,7},{6,8},{7,9},{8,10},{9,11},{10,... | collective-permute-start | bytes 1105928
  1168.2 21.8 %collective-permute-start.14 = (bf16[40,4608]{1,0:T(8,128)(2,1)S(1)}, bf16[40,4608]{1,0:T(8,128)(2,1)S(1)}, u32[]{:S(2)}, u32[]{:S(2)}) collective-permute-start(bf16[40,4608]{1,0:T(8,128)(2,1)S(1)} %get-tuple-element.48), channel_id=1, source_target_pairs={{0,3},{1,4},{2,5},{3,6},{4,7},{5,8},{6,9},{7,10},{8,11},{9,12},{10... | collective-permute-start | bytes 1105928
  1175.5 18.7 %collective-permute-start = (bf16[40,4608]{1,0:T(8,128)(2,1)}, bf16[40,4608]{1,0:T(8,128)(2,1)S(1)}, u32[]{:S(2)}, u32[]{:S(2)}) collective-permute-start(bf16[40,4608]{1,0:T(8,128)(2,1)} %get-tuple-element.47), channel_id=1, source_target_pairs={{0,1},{1,2},{2,3},{3,4},{4,5},{5,6},{6,7},{7,8},{8,9},{9,10},{10,1... | collective-permute-start | bytes 1105928
  1178.2 24.9 %collective-permute-start.1 = (bf16[40,4608]{1,0:T(8,128)(2,1)}, bf16[40,4608]{1,0:T(8,128)(2,1)}, u32[]{:S(2)}, u32[]{:S(2)}) collective-permute-start(bf16[40,4608]{1,0:T(8,128)(2,1)} %get-tuple-element.47), channel_id=1, source_target_pairs={{0,2},{1,3},{2,4},{3,5},{4,6},{5,7},{6,8},{7,9},{8,10},{9,11},{10,... | collective-permute-start | bytes 1105928
  1180.5 65.3 %collective-permute-start.2 = (bf16[40,4608]{1,0:T(8,128)(2,1)}, bf16[40,4608]{1,0:T(8,128)(2,1)}, u32[]{:S(2)}, u32[]{:S(2)}) collective-permute-start(bf16[40,4608]{1,0:T(8,128)(2,1)} %get-tuple-element.47), channel_id=1, source_target_pairs={{0,3},{1,4},{2,5},{3,6},{4,7},{5,8},{6,9},{7,10},{8,11},{9,12},{10... | collective-permute-start | bytes 1105928
  1182.5 80.6 %collective-permute-start.4 = (bf16[40,4608]{1,0:T(8,128)(2,1)S(1)}, bf16[40,4608]{1,0:T(8,128)(2,1)}, u32[]{:S(2)}, u32[]{:S(2)}) collective-permute-start(bf16[40,4608]{1,0:T(8,128)(2,1)S(1)} %get-tuple-element.46), channel_id=1, source_target_pairs={{0,1},{1,2},{2,3},{3,4},{4,5},{5,6},{6,7},{7,8},{8,9},{9,10},{10,1... | collective-permute-start | bytes 1105928
  1190.0 73.1 %collective-permute-start.5 = (bf16[40,4608]{1,0:T(8,128)(2,1)S(1)}, bf16[40,4608]{1,0:T(8,128)(2,1)}, u32[]{:S(2)}, u32[]{:S(2)}) collective-permute-start(bf16[40,4608]{1,0:T(8,128)(2,1)S(1)} %get-tuple-element.46), channel_id=1, source_target_pairs={{0,2},{1,3},{2,4},{3,5},{4,6},{5,7},{6,8},{7,9},{8,10},{9,11},{10,... | collective-permute-start | bytes 1105928
  1194.9 68.2 %collective-permute-start.6 = (bf16[40,4608]{1,0:T(8,128)(2,1)S(1)}, bf16[40,4608]{1,0:T(8,128)(2,1)}, u32[]{:S(2)}, u32[]{:S(2)}) collective-permute-start(bf16[40,4608]{1,0:T(8,128)(2,1)S(1)} %get-tuple-element.46), channel_id=1, source_target_pairs={{0,3},{1,4},{2,5},{3,6},{4,7},{5,8},{6,9},{7,10},{8,11},{9,12},{10... | collective-permute-start | bytes 1105928
  1203.0 60.0 %collective-permute-start.7 = (bf16[4,4608]{1,0:T(4,128)(2,1)S(1)}, bf16[4,4608]{1,0:T(4,128)(2,1)S(1)}, u32[]{:S(2)}, u32[]{:S(2)}) collective-permute-start(bf16[4,4608]{1,0:T(4,128)(2,1)S(1)} %slice.28), channel_id=1, source_target_pairs={{0,4},{1,5},{2,6},{3,7},{4,8},{5,9},{6,10},{7,11},{8,12},{9,13},{1... | collective-permute-start | bytes 110600
  (27 other events, 1901.2 us)
Sparse Core Ops, SparseCore 0:
  11.0 85.4 all-gather.12
  99.3 82.3 all-gather.14
  184.6 57.1 all-gather.16
  244.5 57.2 all-gather.20
  304.5 82.4 all-gather.22
  389.7 82.3 all-gather.18
  645.2 93.3 reduce-scatter.10
  818.8 325.0 reduce-scatter.12
  1286.4 63.5 all-reduce.11
where the time goes:
time: 1460 us; the launch traced here: 1450 us
  matrix products  551 us (38%)
  blocking collectives  358 us (25%)
  waiting for transfers between devices  321 us (22%)
  local copies, waits for them, and re-layouts  108 us (7%)
  starting transfers between devices  69.6 us (5%)
  other arithmetic  24.3 us (2%)
  between operations  17.9 us (1%)
    unnamed x1, blocking collectives  290 us
    all_gather x6, waiting for transfers between devices, fetched(): lax.all_gather(w[number], 's', axis=0, tiled=True)  256 us
    dot_general x5, matrix products, layer(): gate = jnp.dot(a, w['w_gate'], preferred_element_type=jnp.float32)  196 us
    dot_general x5, matrix products, layer(): up = jnp.dot(a, w['w_up'], preferred_element_type=jnp.float32)  194 us
    dot_general x5, matrix products, matmul(): jnp.dot(a, w, preferred_element_type=jnp.float32).astype(jnp.bfloat16)  161 us
    unnamed x69, local copies, waits for them, and re-layouts  92.9 us
    unnamed x16, starting transfers between devices  69 us
    psum x1, blocking collectives, step(): squares = lax.psum(sum((jnp.sum(g * g) for g in gradients)), 's')  67.7 us
  transfers between devices with their start and end apart: 25, of which 7 were waited for; matrix products, arithmetic and copies ran while one was open for 53% of the time, Pallas kernels for 0%

commit v1 on v0

v1 whole, which is shorter than its diff:
```python
import functools

import jax
import jax.numpy as jnp
from jax import lax
from jax.experimental import pallas as pl
from jax.experimental.pallas import tpu as pltpu
from jax.sharding import PartitionSpec as P

BF, F32 = jnp.bfloat16, jnp.float32
S = 32
D, FF, T = 1152, 4608, 2048
C = 1152
Q = FF // C
ROWS = 432
LIMIT = 62 * 1024 * 1024
LAST, FIRST = ((1,), (1,)), ((0,), (0,))


def params(dims):
    return pltpu.CompilerParams(dimension_semantics=("arbitrary",) * dims, vmem_limit_bytes=LIMIT)


def cost(flops, moved):
    return pl.CostEstimate(flops=int(flops), bytes_accessed=int(moved), transcendentals=0)


def dot(a, b):
    return jnp.dot(a, b, preferred_element_type=F32)


def dot_general(a, b, dims):
    return lax.dot_general(a, b, (dims, ((), ())), preferred_element_type=F32)


def assemble(to, main, rest):
    to[0:1024, :] = main[...].reshape(1024, C)
    to[1024:1152, :] = rest[...]


def normed_wide(wide):
    return wide * lax.rsqrt(jnp.mean(wide * wide, -1, keepdims=True) + 1e-6)


def gate_up_kernel(a_ref, g_ref, u_ref, gr_ref, ur_ref, act_ref, wg, wu):
    @pl.when(pl.program_id(1) == 0)
    def _():
        assemble(wg, g_ref, gr_ref)
        assemble(wu, u_ref, ur_ref)

    a = a_ref[...]
    gate, up = dot(a, wg[...]), dot(a, wu[...])
    act_ref[...] = (gate * jax.nn.sigmoid(gate) * up).astype(BF)


def weight_specs():
    return [
        pl.BlockSpec((S, 32, C), lambda q, i: (0, q, 0)),
        pl.BlockSpec((S, 32, C), lambda q, i: (0, Q + q, 0)),
        pl.BlockSpec((128, C), lambda q, i: (q, 0)),
        pl.BlockSpec((128, C), lambda q, i: (Q + q, 0)),
    ]


def gate_up(a, packed, rest, tm=512):
    return pl.pallas_call(
        gate_up_kernel,
        out_shape=jax.ShapeDtypeStruct((T, FF), BF),
        grid=(Q, T // tm),
        in_specs=[pl.BlockSpec((tm, D), lambda q, i: (i, 0))] + weight_specs(),
        out_specs=pl.BlockSpec((tm, C), lambda q, i: (i, q)),
        scratch_shapes=[pltpu.VMEM((D, C), BF)] * 2,
        compiler_params=params(2),
        cost_estimate=cost(4 * T * D * FF, 60e6),
        name="gate_up",
    )(a, packed, packed, rest, rest)


def down_kernel(act_ref, w_ref, x_ref, h_ref, a_ref):
    out = dot(act_ref[...], w_ref[...].reshape(FF, D)).astype(BF)
    h = x_ref[...] + out
    h_ref[...] = h
    a_ref[...] = normed_wide(h.astype(F32)).astype(BF)


def down(act, packed, x, tm=256):
    row = pl.BlockSpec((tm, D), lambda i: (i, 0))
    return pl.pallas_call(
        down_kernel,
        out_shape=(jax.ShapeDtypeStruct((T, D), BF),) * 2,
        grid=(T // tm,),
        in_specs=[pl.BlockSpec((tm, FF), lambda i: (i, 0)), pl.BlockSpec((S, 144, D), lambda i: (0, 2, 0)), row],
        out_specs=(row, row),
        compiler_params=params(1),
        cost_estimate=cost(2 * T * D * FF, 45e6),
        name="down",
    )(act, packed, x)


def back_kernel(with_act, a_ref, dy_ref, g_ref, u_ref, gr_ref, ur_ref, d_ref, *refs):
    if with_act:
        act_ref, dgu_ref, wg, wu = refs
    else:
        dgu_ref, wg, wu = refs

    @pl.when(pl.program_id(1) == 0)
    def _():
        assemble(wg, g_ref, gr_ref)
        assemble(wu, u_ref, ur_ref)

    a = a_ref[...]
    gate, up = dot(a, wg[...]), dot(a, wu[...])
    dact = dot_general(dy_ref[...], d_ref[...].reshape(C, D), LAST).astype(BF).astype(F32)
    sig = jax.nn.sigmoid(gate)
    silu = gate * sig
    if with_act:
        act_ref[...] = (silu * up).astype(BF)
    dgu_ref[0, :, :] = (dact * up * (sig + silu * (1.0 - sig))).astype(BF)
    dgu_ref[1, :, :] = (dact * silu).astype(BF)


def back(a, dy, packed, rest, with_act, tm=512):
    row = pl.BlockSpec((tm, D), lambda q, i: (i, 0))
    shapes = [jax.ShapeDtypeStruct((2, T, FF), BF)]
    specs = [pl.BlockSpec((2, tm, C), lambda q, i: (0, i, q))]
    if with_act:
        shapes.insert(0, jax.ShapeDtypeStruct((T, FF), BF))
        specs.insert(0, pl.BlockSpec((tm, C), lambda q, i: (i, q)))
    out = pl.pallas_call(
        functools.partial(back_kernel, with_act),
        out_shape=tuple(shapes),
        grid=(Q, T // tm),
        in_specs=[row, row] + weight_specs() + [pl.BlockSpec((8, 144, D), lambda q, i: (q, 2, 0))],
        out_specs=tuple(specs),
        scratch_shapes=[pltpu.VMEM((D, C), BF)] * 2,
        compiler_params=params(2),
        cost_estimate=cost(6 * T * D * FF, 130e6),
        name="back",
    )(a, dy, packed, packed, rest, rest, packed)
    return out if with_act else (None, out[0])


def dstate_kernel(dg_ref, du_ref, g_ref, u_ref, gr_ref, ur_ref, h_ref, dy_ref, dh_ref, wg, wu, sg, su, *, tm):
    q, i = pl.program_id(0), pl.program_id(1)

    @pl.when(i == 0)
    def _():
        assemble(wg, g_ref, gr_ref)
        assemble(wu, u_ref, ur_ref)

    rows = pl.ds(pl.multiple_of(i * tm, tm), tm)
    pg, pu = dot_general(dg_ref[0], wg[...], LAST), dot_general(du_ref[0], wu[...], LAST)

    @pl.when(q == 0)
    def _():
        sg[rows, :] = pg
        su[rows, :] = pu

    @pl.when(q > 0)
    def _():
        sg[rows, :] = sg[rows, :] + pg
        su[rows, :] = su[rows, :] + pu

    @pl.when(q == Q - 1)
    def _():
        da = (sg[rows, :].astype(BF) + su[rows, :].astype(BF)).astype(F32)
        wide = h_ref[...].astype(F32)
        scale = lax.rsqrt(jnp.mean(wide * wide, -1, keepdims=True) + 1e-6)
        along = jnp.sum(da * wide, -1, keepdims=True) * (scale * scale * scale) * (1.0 / D)
        dh_ref[...] = dy_ref[...] + (da * scale - wide * along).astype(BF)


def dstate(dgu, packed, rest, h, dy, tm=512):
    last = pl.BlockSpec((tm, D), lambda q, i: (jnp.where(q == Q - 1, i, 0), 0))
    return pl.pallas_call(
        functools.partial(dstate_kernel, tm=tm),
        out_shape=jax.ShapeDtypeStruct((T, D), BF),
        grid=(Q, T // tm),
        in_specs=[pl.BlockSpec((1, tm, C), lambda q, i: (0, i, q)), pl.BlockSpec((1, tm, C), lambda q, i: (1, i, q))]
        + weight_specs()
        + [last, last],
        out_specs=last,
        scratch_shapes=[pltpu.VMEM((D, C), BF)] * 2 + [pltpu.VMEM((T, D), F32)] * 2,
        compiler_params=params(2),
        cost_estimate=cost(4 * T * D * FF, 75e6),
        name="dstate",
    )(dgu, dgu, packed, packed, rest, rest, h, dy)


def d_down_kernel(act_ref, dy_ref, out_ref):
    out_ref[...] = dot_general(act_ref[...], dy_ref[...], FIRST).astype(BF).reshape(8, 144, D)


def d_down(act, dy, alone):
    return pl.pallas_call(
        d_down_kernel,
        out_shape=jax.ShapeDtypeStruct((S, 144 if alone else ROWS, D), BF),
        grid=(Q,),
        in_specs=[pl.BlockSpec((T, C), lambda q: (0, q)), pl.BlockSpec((T, D), lambda q: (0, 0))],
        out_specs=pl.BlockSpec((8, 144, D), lambda q: (q, 0 if alone else 2, 0)),
        compiler_params=params(1),
        cost_estimate=cost(2 * T * D * FF, 35e6),
        name="d_down",
    )(act, dy)


def d_gate_up_kernel(at_ref, dgu_ref, order_ref, *refs):
    out_ref, rest = refs[-2:]
    g = pl.program_id(0)

    @pl.when(g < 2 * Q)
    def _():
        term = dot(at_ref[...], dgu_ref[0]).astype(BF)
        out_ref[...] = term[0:1024, :].reshape(S, 32, C)
        rest[pl.ds(pl.multiple_of(g * 128, 128), 128), :] = term[1024:1152, :]

    @pl.when(g == 2 * Q)
    def _():
        out_ref[...] = dot(order_ref[...], rest[...]).astype(BF).reshape(S, 32, C)


def d_gate_up(at, dgu, order, packed=None):
    def block(g):
        g = jnp.minimum(g, 2 * Q - 1)
        return (g // Q, 0, g % Q)

    return pl.pallas_call(
        d_gate_up_kernel,
        out_shape=jax.ShapeDtypeStruct((S, 288 if packed is None else ROWS, D), BF),
        grid=(2 * Q + 1,),
        in_specs=[
            pl.BlockSpec((D, T), lambda g: (0, 0)),
            pl.BlockSpec((1, T, C), block),
            pl.BlockSpec((1024, 1024), lambda g: (0, 0)),
        ]
        + [pl.BlockSpec(memory_space=pl.ANY)] * (packed is not None),
        out_specs=pl.BlockSpec((S, 32, C), lambda g: (0, g, 0)),
        scratch_shapes=[pltpu.VMEM((1024, C), BF)],
        input_output_aliases={} if packed is None else {3: 0},
        compiler_params=params(1),
        cost_estimate=cost(4 * T * D * FF, 65e6),
        name="d_gate_up",
    )(at, dgu, order, *([] if packed is None else [packed]))


def total_kernel(part_ref, out_ref, mine, slots, send, recv):
    me = lax.axis_index("s")
    y, z, core = me // 8, (me // 2) % 4, me % 2
    stages = [
        [y * 8 + z * 2 + (1 - core)],
        [y * 8 + ((z + k) % 4) * 2 + core for k in (1, 2, 3)],
        [((y + k) % 4) * 8 + z * 2 + core for k in (1, 2, 3)],
    ]
    barrier = pltpu.get_barrier_semaphore()
    for peers in stages:
        for peer in peers:
            pl.semaphore_signal(barrier, inc=1, device_id={"s": peer}, device_id_type=pl.DeviceIdType.MESH)
    pl.semaphore_wait(barrier, 7)
    total, slot = part_ref[...], 0
    for number, peers in enumerate(stages):
        mine[number] = total
        copies = []
        for peer in peers:
            copy = pltpu.make_async_remote_copy(
                src_ref=mine.at[number],
                dst_ref=slots.at[slot],
                send_sem=send.at[slot],
                recv_sem=recv.at[slot],
                device_id={"s": peer},
                device_id_type=pl.DeviceIdType.MESH,
            )
            copy.start()
            copies.append((copy, slot))
            slot += 1
        for copy, at in copies:
            copy.wait()
            total = total + slots[at]
    out_ref[...] = total


def summed_over_group(part):
    block = jnp.where(lax.broadcasted_iota(jnp.int32, (8, 128), 0) + lax.broadcasted_iota(jnp.int32, (8, 128), 1) == 0, part, 0.0)
    return pl.pallas_call(
        total_kernel,
        out_shape=jax.ShapeDtypeStruct((8, 128), F32),
        in_specs=[pl.BlockSpec(memory_space=pltpu.VMEM)],
        out_specs=pl.BlockSpec(memory_space=pltpu.VMEM),
        scratch_shapes=[
            pltpu.VMEM((3, 8, 128), F32),
            pltpu.VMEM((7, 8, 128), F32),
            pltpu.SemaphoreType.DMA((7,)),
            pltpu.SemaphoreType.DMA((7,)),
        ],
        compiler_params=pltpu.CompilerParams(collective_id=0, has_side_effects=True),
        name="total",
    )(block)[0, 0]


def one_hot(rows, columns):
    return (rows[:, None] == columns[None, :]).astype(BF)


def feature_order():
    j = jnp.arange(D, dtype=jnp.int32)
    k = j - 1024
    return one_hot(j, jnp.where(j < 1024, (j // 32) * 36 + j % 32, (k // 4) * 36 + 32 + k % 4))


def rest_order():
    p, t = (jnp.arange(1024, dtype=jnp.int32) for _ in range(2))
    return one_hot((p % 32 // 4) * 128 + (p // 32) * 4 + p % 4, t)


def moved(a, order):
    return jnp.dot(a, order, preferred_element_type=F32).astype(BF)


def pack(gate, up, dn, order):
    main = [w[:32].reshape(32, Q, C).transpose(1, 0, 2).reshape(128, C) for w in (gate, up)]
    rest = [w[32:].reshape(4, Q, C).transpose(1, 0, 2).reshape(16, C) for w in (gate, up)]
    return jnp.concatenate(main + rest + [moved(dn, order)])


def unpack(g, order):
    out = []
    for i in range(2):
        main = g[128 * i : 128 * i + 128].reshape(Q, 32, C).transpose(1, 0, 2).reshape(32, FF)
        rest = g[256 + 16 * i : 272 + 16 * i].reshape(Q, 4, C).transpose(1, 0, 2).reshape(4, FF)
        out.append(jnp.concatenate([main, rest]))
    return out + [moved(g[288:], order.T)]


def adamw(w, m, v, g):
    m = 0.9 * m + 0.1 * g
    v = 0.95 * v + 0.05 * g * g
    step = m * lax.rsqrt(v + 1e-8) + 0.1 * w
    return (w - 0.02 * step).astype(BF), m, v


def across(block, n=4):
    total = block.astype(F32)
    for shift in range(1, n):
        total = total + lax.ppermute(block, "r", [(i, (i + shift) % n) for i in range(n)]).astype(F32)
    return total.astype(BF)


def scattered(term):
    return lax.psum_scatter(term.reshape(-1, C), "s", scatter_dimension=0, tiled=True)


def rest_of(packed, rests):
    return moved(rests.T, packed[:, 256:288, :].reshape(1024, C))


def solution(mesh):
    def step(x, dy, *arrays):
        weights, m, v = (arrays[i : i + 3] for i in (0, 3, 6))
        order, rests = feature_order(), rest_order()

        packed = [
            lax.all_gather(pack(*(w[n] for w in weights), order), "s", axis=0, tiled=True).reshape(S, ROWS, C)
            for n in range(2)
        ]

        x, dy = moved(x[0], order), moved(dy[0], order)
        a0 = normed_wide(x.astype(F32)).astype(BF)
        at0 = a0.T
        rest = [rest_of(packed[0], rests)]
        act0 = gate_up(a0, packed[0], rest[0])
        h1, a1 = down(act0, packed[0], x)
        a1, packed[1] = lax.optimization_barrier((a1, packed[1]))
        rest.append(rest_of(packed[1], rests))
        at1 = a1.T
        act1, dgu1 = back(a1, dy, packed[1], rest[1], True)
        term1 = d_gate_up(at1, dgu1, rests, d_down(act1, dy, False))
        term1, dgu1 = lax.optimization_barrier((term1, dgu1))
        sum1 = scattered(term1)
        dh1 = dstate(dgu1, packed[1], rest[1], h1, dy)
        down0, dh1 = lax.optimization_barrier((d_down(act0, dh1, True), dh1))
        sum_down0 = scattered(down0)
        _, dgu0 = back(a0, dh1, packed[0], rest[0], False)
        sum0 = scattered(d_gate_up(at0, dgu0, rests))

        blocks = [across(b) for b in (sum0, sum_down0, sum1)]
        squares = summed_over_group(sum(jnp.sum(jnp.square(b.astype(F32))) for b in blocks))
        blocks = [jnp.concatenate(blocks[:2]), blocks[2]]
        factor = jnp.minimum(1.0, 0.5 * lax.rsqrt(squares / (2 * 3 * D * FF) + 1e-30))
        pieces = [unpack(b, order) for b in blocks]
        new = [
            adamw(weights[i].astype(F32), m[i], v[i], jnp.stack([pieces[n][i] for n in range(2)]).astype(F32) * factor)
            for i in range(3)
        ]
        return tuple(one[which] for which in range(3) for one in new)

    states, cut = P(("rep", "r", "s"), None, None), P(None, "s", None)
    return jax.shard_map(
        step,
        mesh=mesh,
        in_specs=(states, states) + (cut,) * 9,
        out_specs=(P("rep", "s", None),) * 9,
        check_vma=False,
    )
```

time: 1460 us -> 1100 us (0.75)
  Pallas kernels: 0 us -> 552 us
  matrix products: 551 us -> 35.5 us
  blocking collectives: 358 us -> 0 us
  waiting for transfers between devices: 321 us -> 393 us
  starting transfers between devices: 69.6 us -> 13.9 us
  local copies, waits for them, and re-layouts: 108 us -> 53.2 us
    pallas_call x0 -> x10, Pallas kernels: none -> 552 us  [the longest x2 189 us: back(): pl.pallas_call(functools.partial(back_kernel, with_act), out_shape=tuple(...]
    dot_general x15 -> x8, matrix products: 551 us -> 35.5 us  [moved(): return jnp.dot(a, order, preferred_element_type=F32).astype(BF)]
    unnamed x1 -> x0, blocking collectives: 290 us -> none
    all_gather x6 -> x2, waiting for transfers between devices: 256 us -> 75.8 us  [step(): lax.all_gather(pack(*(w[n] for w in weights), order), 's', axis=0, tiled=...]
    reduce_scatter x2, waiting for transfers between devices: 0.01 us -> 123 us  [scattered(): lax.psum_scatter(term.reshape(-1, C), 's', scatter_dimension=0, tiled=True)]
    unnamed x25 -> x6, waiting for transfers between devices: 1.72 us -> 125 us
    unnamed x69 -> x62, local copies, waits for them, and re-layouts: 92.9 us -> 15.7 us
    ppermute x0 -> x9, waiting for transfers between devices: none -> 69 us  [across(): lax.ppermute(block, 'r', [(i, (i + shift) % n) for i in range(n)])]
  transfers between devices with their start and end apart: 25 -> 14, of which waited for: 7 -> 8; matrix products, arithmetic and copies ran while one was open for 53% -> 6% of each run, Pallas kernels for 0% -> 23%
where the time goes in v1:
time: 1100 us; the launch traced here: 1090 us
  Pallas kernels  552 us (50%)
  waiting for transfers between devices  393 us (36%)
  local copies, waits for them, and re-layouts  53.2 us (5%)
  matrix products  35.5 us (3%)
  other arithmetic  23.9 us (2%)
  between operations  17.4 us (2%)
  starting transfers between devices  13.9 us (1%)
    pallas_call x2, Pallas kernels, back(): pl.pallas_call(functools.partial(back_kernel, with_act), out_shape=tuple(...  189 us
    unnamed x6, waiting for transfers between devices  125 us
    reduce_scatter x2, waiting for transfers between devices, scattered(): lax.psum_scatter(term.reshape(-1, C), 's', scatter_dimension=0, tiled=True)  123 us
    pallas_call x2, Pallas kernels, d_gate_up(): pl.pallas_call(d_gate_up_kernel, out_shape=jax.ShapeDtypeStruct((S, 288 i...  119 us
    all_gather x2, waiting for transfers between devices, step(): lax.all_gather(pack(*(w[n] for w in weights), order), 's', axis=0, tiled=...  75.8 us
    pallas_call x1, Pallas kernels, dstate(): pl.pallas_call(functools.partial(dstate_kernel, tm=tm), out_shape=jax.Sha...  75.7 us
    ppermute x9, waiting for transfers between devices, across(): lax.ppermute(block, 'r', [(i, (i + shift) % n) for i in range(n)])  69 us
    pallas_call x1, Pallas kernels, gate_up(): pl.pallas_call(gate_up_kernel, out_shape=jax.ShapeDtypeStruct((T, FF), BF...  62.7 us
  transfers between devices with their start and end apart: 14, of which 8 were waited for; matrix products, arithmetic and copies ran while one was open for 6% of the time, Pallas kernels for 23%

profile of v1, /device:TPU:0, one launch (start us, length us, event | category | flops | bytes accessed | tf_op | source)
XLA Modules:
  0.0 1088.6 jit_solution(9719551171279144633)
XLA Ops:
  21.7 10.3 fusion
  31.9 6.7 copy.82.x_ref
  39.3 6.1 fusion.1
  45.4 6.7 copy.89.a_ref
  53.8 10.3 fusion.2.dy_ref
  64.1 66.3 %all-gather.3.cloned.1.call-done = bf16[13824,1152]{1,0:T(8,128)(2,1)} async-done(((bf16[432,1152]{1,0:T(8,128)(2,1)}), bf16[13824,1152]{1,0:T(8,128)(2,1)}) %all-gather.3.cloned.1.call-update) | async-done | bytes 31850512 | tf_op jit(solution)/shard_map/all_gather | solution.py:361
  136.7 62.7 %gate_up.1.act_ref = bf16[2048,4608]{1,0:T(8,128)(2,1)} custom-call(bf16[2048,1152]{1,0:T(8,128)(2,1)} %copy.89.a_ref, bf16[32,432,1152]{2,1,0:T(8,128)(2,1)} %bitcast.128, bf16[32,432,1152]{2,1,0:T(8,128)(2,1)} %bitcast.129, bf16[1024,1152]{1,0:T(8,128)(2,1)} %fusion.13.gr_ref.ur_ref, bf16[1024,1152]{1,0:T(8,128)(2,1)} %fusion.13.gr_ref.ur_ref), custom_call_target="tpu_custom_call" | custom-call | flops 43486543872 | bytes 60000000 | tf_op jit(solution)/shard_map/gate_up/pallas_call | solution.py:66
  199.4 32.6 %down.1 = (bf16[2048,1152]{1,0:T(8,128)(2,1)}, bf16[2048,1152]{1,0:T(8,128)(2,1)}) custom-call(bf16[2048,4608]{1,0:T(8,128)(2,1)} %gate_up.1.act_ref, bf16[32,432,1152]{2,1,0:T(8,128)(2,1)} %bitcast.130, bf16[2048,1152]{1,0:T(8,128)(2,1)} %copy.82.x_ref), custom_call_target="tpu_custom_call" | custom-call | flops 21743271936 | bytes 45000000 | tf_op jit(solution)/shard_map/down/pallas_call | solution.py:88
  232.1 9.5 all-gather.5.cloned.1.call-done
  243.4 4.4 fusion.14.gr_ref.ur_ref
  247.9 6.7 copy.87
  254.6 95.8 %back.2 = (bf16[2048,4608]{1,0:T(8,128)(2,1)}, bf16[2,2048,4608]{2,1,0:T(8,128)(2,1)}) custom-call(bf16[2048,1152]{1,0:T(8,128)(2,1)} %get-tuple-element.20.a_ref, bf16[2048,1152]{1,0:T(8,128)(2,1)} %fusion.2.dy_ref, bf16[32,432,1152]{2,1,0:T(8,128)(2,1)} %bitcast.135, bf16[32,432,1152]{2,1,0:T(8,128)(2,1)} %bitcast.136, ...), custom_call_target="tpu_custom_call" | custom-call | flops 65229815808 | bytes 130000000 | tf_op jit(solution)/shard_map/back/pallas_call | solution.py:129
  350.4 30.9 %d_down.2.refs_0_ = bf16[32,432,1152]{2,1,0:T(8,128)(2,1)} custom-call(bf16[2048,4608]{1,0:T(8,128)(2,1)} %get-tuple-element.23.act_ref, bf16[2048,1152]{1,0:T(8,128)(2,1)} %fusion.2.dy_ref), custom_call_target="tpu_custom_call" | custom-call | flops 21743271936 | bytes 35000000 | tf_op jit(solution)/shard_map/d_down/pallas_call | solution.py:195
  381.3 59.5 %d_gate_up.2 = bf16[32,432,1152]{2,1,0:T(8,128)(2,1)} custom-call(bf16[1152,2048]{1,0:T(8,128)(2,1)} %bitcast.104, bf16[2,2048,4608]{2,1,0:T(8,128)(2,1)} %get-tuple-element.24.dgu_ref.dg_ref.du_ref, bf16[1024,1024]{1,0:T(8,128)(2,1)} %fusion.10.order_ref, bf16[32,432,1152]{2,1,0:T(8,128)(2,1)} %d_down.2.refs_0_), custom_call_target="tpu_custom_call", output_to_operand_aliasing={{}: (3, {})} | custom-call | flops 43486543872 | bytes 65000000 | tf_op jit(solution)/shard_map/d_gate_up/pallas_call | solution.py:227
  440.8 75.7 %dstate.1.dy_ref = bf16[2048,1152]{1,0:T(8,128)(2,1)} custom-call(bf16[2,2048,4608]{2,1,0:T(8,128)(2,1)} %get-tuple-element.24.dgu_ref.dg_ref.du_ref, bf16[2,2048,4608]{2,1,0:T(8,128)(2,1)} %get-tuple-element.24.dgu_ref.dg_ref.du_ref, bf16[32,432,1152]{2,1,0:T(8,128)(2,1)} %bitcast.138, bf16[32,432,1152]{2,1,0:T(8,128)(2,1)} %bitcast.139, ...), custom_call_target="tpu_custom_call" | custom-call | flops 43486543872 | bytes 75000000 | tf_op jit(solution)/shard_map/dstate/pallas_call | solution.py:175
  516.4 30.8 %d_down.3 = bf16[32,144,1152]{2,1,0:T(8,128)(2,1)} custom-call(bf16[2048,4608]{1,0:T(8,128)(2,1)} %gate_up.1.act_ref, bf16[2048,1152]{1,0:T(8,128)(2,1)} %dstate.1.dy_ref), custom_call_target="tpu_custom_call" | custom-call | flops 21743271936 | bytes 35000000 | tf_op jit(solution)/shard_map/d_down/pallas_call | solution.py:195
  547.9 6.1 multiply_convert_fusion.at_ref
  554.0 93.2 %back.3.dgu_ref = bf16[2,2048,4608]{2,1,0:T(8,128)(2,1)} custom-call(bf16[2048,1152]{1,0:T(8,128)(2,1)} %copy.89.a_ref, bf16[2048,1152]{1,0:T(8,128)(2,1)} %dstate.1.dy_ref, bf16[32,432,1152]{2,1,0:T(8,128)(2,1)} %bitcast.131, bf16[32,432,1152]{2,1,0:T(8,128)(2,1)} %bitcast.132, bf16[1024,1152]{1,0:T(8,128)(2,1)} %fusion.13.gr_ref.ur_ref, ...), custom_call_target="tpu_custom_call" | custom-call | flops 65229815808 | bytes 130000000 | tf_op jit(solution)/shard_map/back/pallas_call | solution.py:129
  647.2 59.5 %d_gate_up.3 = bf16[32,288,1152]{2,1,0:T(8,128)(2,1)} custom-call(bf16[1152,2048]{1,0:T(8,128)(2,1)} %multiply_convert_fusion.at_ref, bf16[2,2048,4608]{2,1,0:T(8,128)(2,1)} %back.3.dgu_ref, bf16[1024,1024]{1,0:T(8,128)(2,1)} %fusion.10.order_ref), custom_call_target="tpu_custom_call" | custom-call | flops 43486543872 | bytes 65000000 | tf_op jit(solution)/shard_map/d_gate_up/pallas_call | solution.py:227
  711.8 123.5 %reduce-scatter.6.cloned.1.call-done = bf16[288,1152]{1,0:T(8,128)(2,1)} async-done(((bf16[9216,1152]{1,0:T(8,128)(2,1)}), bf16[288,1152]{1,0:T(8,128)(2,1)}) %reduce-scatter.6.cloned.1.call-update) | async-done | bytes 663568 | tf_op jit(solution)/shard_map/reduce_scatter | solution.py:348
  843.4 22.0 %collective-permute-done.2 = bf16[288,1152]{1,0:T(8,128)(2,1)S(1)} collective-permute-done((bf16[288,1152]{1,0:T(8,128)(2,1)}, bf16[288,1152]{1,0:T(8,128)(2,1)S(1)}, u32[]{:S(2)}, u32[]{:S(2)}) %collective-permute-start.2) | collective-permute-done | bytes 663584 | tf_op jit(solution)/shard_map/ppermute | solution.py:343
  871.7 123.9 %reduce-scatter.10.cloned.1.call-done = bf16[432,1152]{1,0:T(8,128)(2,1)} async-done(((bf16[13824,1152]{1,0:T(8,128)(2,1)}), bf16[432,1152]{1,0:T(8,128)(2,1)}) %reduce-scatter.10.cloned.1.call-update) | async-done | bytes 995344
  1000.3 40.0 %collective-permute-done.5 = bf16[432,1152]{1,0:T(8,128)(2,1)S(1)} collective-permute-done((bf16[432,1152]{1,0:T(8,128)(2,1)}, bf16[432,1152]{1,0:T(8,128)(2,1)S(1)}, u32[]{:S(2)}, u32[]{:S(2)}) %collective-permute-start.5) | collective-permute-done | bytes 995360 | tf_op jit(solution)/shard_map/ppermute | solution.py:343
  1049.1 11.3 %total.1 = f32[8,128]{1,0:T(8,128)} custom-call(f32[8,128]{1,0:T(8,128)} %fusion.94.part_ref), custom_call_target="tpu_custom_call" | custom-call | tf_op jit(solution)/shard_map/total/pallas_call | solution.py:283
  (151 shorter events, 76.7 us)
Async XLA Ops:
  7.2 5.2 copy-start.1
  7.2 123.2 %all-gather.3.cloned.1.call-start = ((), (), s32[]{:S(2)}) async-start(), calls=%async_computation.3 | async-start | bytes 32845824 | tf_op jit(solution)/shard_map/all_gather | solution.py:361
  7.2 46.6 %copy-start.18 = (s32[1152]{0:T(1024)}, s32[1152]{0:T(1024)S(1)}, u32[]{:S(2)}) copy-start(s32[1152]{0:T(1024)S(1)} %fusion.73) | copy-start | bytes 13828
  18.7 222.9 %all-gather.5.cloned.1.call-start = ((), (), s32[]{:S(2)}) async-start(), calls=%async_computation.4 | async-start | bytes 32845824 | tf_op jit(solution)/shard_map/all_gather | solution.py:361
  21.4 685.9 %reduce-scatter.8.cloned.1.call-start = ((), (), s32[]{:S(2)}) async-start(), calls=%async_computation.6 | async-start | bytes 10948608 | tf_op jit(solution)/shard_map/reduce_scatter | solution.py:348
  547.2 288.1 %reduce-scatter.6.cloned.1.call-start = ((), (), s32[]{:S(2)}) async-start(), calls=%async_computation.5 | async-start | bytes 21897216 | tf_op jit(solution)/shard_map/reduce_scatter | solution.py:348
  706.7 289.0 %reduce-scatter.10.cloned.1.call-start = ((), (), s32[]{:S(2)}) async-start(), calls=%async_computation.7 | async-start | bytes 32845824
  707.3 134.2 %copy-start.19 = (s32[1152]{0:T(1024)S(1)}, s32[1152]{0:T(1024)}, u32[]{:S(2)}) copy-start(s32[1152]{0:T(1024)} %copy-done.18) | copy-start | bytes 13828
  707.3 131.5 %collective-permute-start.8 = (bf16[144,1152]{1,0:T(8,128)(2,1)}, bf16[144,1152]{1,0:T(8,128)(2,1)S(1)}, u32[]{:S(2)}, u32[]{:S(2)}) collective-permute-start(bf16[144,1152]{1,0:T(8,128)(2,1)} %reduce-scatter.8.cloned.1.call-done), channel_id=1, source_target_pairs={{0,96},{32,0},{64,32},{96,64},{1,97},{33,1},{65,33},{97,65},{2,98}... | collective-permute-start | bytes 995336 | tf_op jit(solution)/shard_map/ppermute | solution.py:343
  710.1 129.6 %collective-permute-start.7 = (bf16[144,1152]{1,0:T(8,128)(2,1)}, bf16[144,1152]{1,0:T(8,128)(2,1)S(1)}, u32[]{:S(2)}, u32[]{:S(2)}) collective-permute-start(bf16[144,1152]{1,0:T(8,128)(2,1)} %reduce-scatter.8.cloned.1.call-done), channel_id=1, source_target_pairs={{0,64},{32,96},{64,0},{96,32},{1,65},{33,97},{65,1},{97,33},{2,66}... | collective-permute-start | bytes 995336 | tf_op jit(solution)/shard_map/ppermute | solution.py:343
  710.9 128.7 %collective-permute-start.6 = (bf16[144,1152]{1,0:T(8,128)(2,1)}, bf16[144,1152]{1,0:T(8,128)(2,1)S(1)}, u32[]{:S(2)}, u32[]{:S(2)}) collective-permute-start(bf16[144,1152]{1,0:T(8,128)(2,1)} %reduce-scatter.8.cloned.1.call-done), channel_id=1, source_target_pairs={{0,32},{32,64},{64,96},{96,0},{1,33},{33,65},{65,97},{97,1},{2,34}... | collective-permute-start | bytes 995336 | tf_op jit(solution)/shard_map/ppermute | solution.py:343
  835.3 30.0 %collective-permute-start.2 = (bf16[288,1152]{1,0:T(8,128)(2,1)}, bf16[288,1152]{1,0:T(8,128)(2,1)S(1)}, u32[]{:S(2)}, u32[]{:S(2)}) collective-permute-start(bf16[288,1152]{1,0:T(8,128)(2,1)} %reduce-scatter.6.cloned.1.call-done), channel_id=1, source_target_pairs={{0,96},{32,0},{64,32},{96,64},{1,97},{33,1},{65,33},{97,65},{2,98}... | collective-permute-start | bytes 1990664 | tf_op jit(solution)/shard_map/ppermute | solution.py:343
  838.0 27.3 %collective-permute-start.1 = (bf16[288,1152]{1,0:T(8,128)(2,1)}, bf16[288,1152]{1,0:T(8,128)(2,1)S(1)}, u32[]{:S(2)}, u32[]{:S(2)}) collective-permute-start(bf16[288,1152]{1,0:T(8,128)(2,1)} %reduce-scatter.6.cloned.1.call-done), channel_id=1, source_target_pairs={{0,64},{32,96},{64,0},{96,32},{1,65},{33,97},{65,1},{97,33},{2,66}... | collective-permute-start | bytes 1990664 | tf_op jit(solution)/shard_map/ppermute | solution.py:343
  838.9 30.0 %collective-permute-start = (bf16[288,1152]{1,0:T(8,128)(2,1)}, bf16[288,1152]{1,0:T(8,128)(2,1)S(1)}, u32[]{:S(2)}, u32[]{:S(2)}) collective-permute-start(bf16[288,1152]{1,0:T(8,128)(2,1)} %reduce-scatter.6.cloned.1.call-done), channel_id=1, source_target_pairs={{0,32},{32,64},{64,96},{96,0},{1,33},{33,65},{65,97},{97,1},{2,34}... | collective-permute-start | bytes 1990664 | tf_op jit(solution)/shard_map/ppermute | solution.py:343
  841.5 27.3 %copy-start.13 = (bf16[288,1152]{1,0:T(8,128)(2,1)S(1)}, bf16[288,1152]{1,0:T(8,128)(2,1)}, u32[]{:S(2)}) copy-start(bf16[288,1152]{1,0:T(8,128)(2,1)} %reduce-scatter.6.cloned.1.call-done) | copy-start | bytes 1990660
  995.7 48.2 %copy-start.10 = (bf16[432,1152]{1,0:T(8,128)(2,1)S(1)}, bf16[432,1152]{1,0:T(8,128)(2,1)}, u32[]{:S(2)}) copy-start(bf16[432,1152]{1,0:T(8,128)(2,1)} %reduce-scatter.10.cloned.1.call-done) | copy-start | bytes 2985988
  995.7 44.7 %collective-permute-start.5 = (bf16[432,1152]{1,0:T(8,128)(2,1)}, bf16[432,1152]{1,0:T(8,128)(2,1)S(1)}, u32[]{:S(2)}, u32[]{:S(2)}) collective-permute-start(bf16[432,1152]{1,0:T(8,128)(2,1)} %reduce-scatter.10.cloned.1.call-done), channel_id=1, source_target_pairs={{0,96},{32,0},{64,32},{96,64},{1,97},{33,1},{65,33},{97,65},{2,98}... | collective-permute-start | bytes 2985992 | tf_op jit(solution)/shard_map/ppermute | solution.py:343
  998.4 42.0 %collective-permute-start.4 = (bf16[432,1152]{1,0:T(8,128)(2,1)}, bf16[432,1152]{1,0:T(8,128)(2,1)S(1)}, u32[]{:S(2)}, u32[]{:S(2)}) collective-permute-start(bf16[432,1152]{1,0:T(8,128)(2,1)} %reduce-scatter.10.cloned.1.call-done), channel_id=1, source_target_pairs={{0,64},{32,96},{64,0},{96,32},{1,65},{33,97},{65,1},{97,33},{2,66}... | collective-permute-start | bytes 2985992 | tf_op jit(solution)/shard_map/ppermute | solution.py:343
  999.2 44.7 %collective-permute-start.3 = (bf16[432,1152]{1,0:T(8,128)(2,1)}, bf16[432,1152]{1,0:T(8,128)(2,1)S(1)}, u32[]{:S(2)}, u32[]{:S(2)}) collective-permute-start(bf16[432,1152]{1,0:T(8,128)(2,1)} %reduce-scatter.10.cloned.1.call-done), channel_id=1, source_target_pairs={{0,32},{32,64},{64,96},{96,0},{1,33},{33,65},{65,97},{97,1},{2,34}... | collective-permute-start | bytes 2985992 | tf_op jit(solution)/shard_map/ppermute | solution.py:343
  1043.9 21.2 %copy-start.9 = (f32[2,36,4608]{2,0,1:T(2,128)S(1)}, f32[2,36,4608]{2,0,1:T(2,128)}, u32[]{:S(2)}) copy-start(f32[2,36,4608]{2,0,1:T(2,128)} %param.20) | copy-start | bytes 3981316
  1062.4 2.8 copy-start.8
  1075.4 4.2 copy-start.12
  1075.4 4.2 copy-start.14
  1075.4 4.2 copy-start.15
  (10 other events, 13.3 us)
Sparse Core Ops, SparseCore 0:
  18.8 111.5 all-gather.2
  133.3 108.2 all-gather.4
  547.3 93.2 reduce-scatter.7
  706.8 128.4 reduce-scatter.5
  839.1 156.5 reduce-scatter.9

commit v2 on v1

--- a/solution.py
+++ b/solution.py
@@ -6,6 +6,7 @@
 from jax.experimental import pallas as pl
 from jax.experimental.pallas import tpu as pltpu
 from jax.sharding import PartitionSpec as P
+
 
 BF, F32 = jnp.bfloat16, jnp.float32
 S = 32
@@ -14,6 +15,7 @@
 Q = FF // C
 ROWS = 432
 LIMIT = 62 * 1024 * 1024
+CUTS = ((0, 512), (512, 1152))
 LAST, FIRST = ((1,), (1,)), ((0,), (0,))
 
 
@@ -49,8 +51,9 @@
         assemble(wu, u_ref, ur_ref)
 
     a = a_ref[...]
-    gate, up = dot(a, wg[...]), dot(a, wu[...])
-    act_ref[...] = (gate * jax.nn.sigmoid(gate) * up).astype(BF)
+    for at, to in CUTS:
+        gate, up = dot(a, wg[:, at:to]), dot(a, wu[:, at:to])
+        act_ref[:, at:to] = (gate * jax.nn.sigmoid(gate) * up).astype(BF)
 
 
 def weight_specs():
@@ -99,24 +102,26 @@
 
 def back_kernel(with_act, a_ref, dy_ref, g_ref, u_ref, gr_ref, ur_ref, d_ref, *refs):
     if with_act:
-        act_ref, dgu_ref, wg, wu = refs
+        act_ref, dgu_ref, wg, wu, wd = refs
     else:
-        dgu_ref, wg, wu = refs
+        dgu_ref, wg, wu, wd = refs
 
     @pl.when(pl.program_id(1) == 0)
     def _():
         assemble(wg, g_ref, gr_ref)
         assemble(wu, u_ref, ur_ref)
-
-    a = a_ref[...]
-    gate, up = dot(a, wg[...]), dot(a, wu[...])
-    dact = dot_general(dy_ref[...], d_ref[...].reshape(C, D), LAST).astype(BF).astype(F32)
-    sig = jax.nn.sigmoid(gate)
-    silu = gate * sig
-    if with_act:
-        act_ref[...] = (silu * up).astype(BF)
-    dgu_ref[0, :, :] = (dact * up * (sig + silu * (1.0 - sig))).astype(BF)
-    dgu_ref[1, :, :] = (dact * silu).astype(BF)
+        wd[...] = d_ref[...].reshape(C, D)
+
+    a, dy = a_ref[...], dy_ref[...]
+    for at, to in CUTS:
+        gate, up = dot(a, wg[:, at:to]), dot(a, wu[:, at:to])
+        dact = dot_general(dy, wd[at:to, :], LAST).astype(BF).astype(F32)
+        sig = jax.nn.sigmoid(gate)
+        silu = gate * sig
+        if with_act:
+            act_ref[:, at:to] = (silu * up).astype(BF)
+        dgu_ref[0, :, at:to] = (dact * up * (sig + silu * (1.0 - sig))).astype(BF)
+        dgu_ref[1, :, at:to] = (dact * silu).astype(BF)
 
 
 def back(a, dy, packed, rest, with_act, tm=512):
@@ -132,7 +137,7 @@
         grid=(Q, T // tm),
         in_specs=[row, row] + weight_specs() + [pl.BlockSpec((8, 144, D), lambda q, i: (q, 2, 0))],
         out_specs=tuple(specs),
-        scratch_shapes=[pltpu.VMEM((D, C), BF)] * 2,
+        scratch_shapes=[pltpu.VMEM((D, C), BF)] * 3,
         compiler_params=params(2),
         cost_estimate=cost(6 * T * D * FF, 130e6),
         name="back",
@@ -140,72 +145,64 @@
     return out if with_act else (None, out[0])
 
 
-def dstate_kernel(dg_ref, du_ref, g_ref, u_ref, gr_ref, ur_ref, h_ref, dy_ref, dh_ref, wg, wu, sg, su, *, tm):
-    q, i = pl.program_id(0), pl.program_id(1)
-
-    @pl.when(i == 0)
+def dstate_kernel(dg_ref, du_ref, g_ref, r_ref, h_ref, dy_ref, dh_ref, wg, wu):
+    @pl.when(pl.program_id(0) == 0)
     def _():
-        assemble(wg, g_ref, gr_ref)
-        assemble(wu, u_ref, ur_ref)
-
-    rows = pl.ds(pl.multiple_of(i * tm, tm), tm)
+        for q in range(Q):
+            cols = slice(q * C, (q + 1) * C)
+            wg[0:1024, cols] = g_ref[:, 32 * q : 32 * q + 32, :].reshape(1024, C)
+            wu[0:1024, cols] = g_ref[:, 128 + 32 * q : 160 + 32 * q, :].reshape(1024, C)
+            wg[1024:1152, cols] = r_ref[128 * q : 128 * q + 128, :]
+            wu[1024:1152, cols] = r_ref[512 + 128 * q : 640 + 128 * q, :]
+
     pg, pu = dot_general(dg_ref[0], wg[...], LAST), dot_general(du_ref[0], wu[...], LAST)
-
-    @pl.when(q == 0)
-    def _():
-        sg[rows, :] = pg
-        su[rows, :] = pu
-
-    @pl.when(q > 0)
-    def _():
-        sg[rows, :] = sg[rows, :] + pg
-        su[rows, :] = su[rows, :] + pu
-
-    @pl.when(q == Q - 1)
-    def _():
-        da = (sg[rows, :].astype(BF) + su[rows, :].astype(BF)).astype(F32)
-        wide = h_ref[...].astype(F32)
-        scale = lax.rsqrt(jnp.mean(wide * wide, -1, keepdims=True) + 1e-6)
-        along = jnp.sum(da * wide, -1, keepdims=True) * (scale * scale * scale) * (1.0 / D)
-        dh_ref[...] = dy_ref[...] + (da * scale - wide * along).astype(BF)
-
-
-def dstate(dgu, packed, rest, h, dy, tm=512):
-    last = pl.BlockSpec((tm, D), lambda q, i: (jnp.where(q == Q - 1, i, 0), 0))
-    return pl.pallas_call(
-        functools.partial(dstate_kernel, tm=tm),
+    da = (pg.astype(BF) + pu.astype(BF)).astype(F32)
+    wide = h_ref[...].astype(F32)
+    scale = lax.rsqrt(jnp.mean(wide * wide, -1, keepdims=True) + 1e-6)
+    along = jnp.sum(da * wide, -1, keepdims=True) * (scale * scale * scale) * (1.0 / D)
+    dh_ref[...] = dy_ref[...] + (da * scale - wide * along).astype(BF)
+
+
+def dstate(dgu, packed, rest, h, dy, tm=256):
+    row = pl.BlockSpec((tm, D), lambda i: (i, 0))
+    return pl.pallas_call(
+        dstate_kernel,
         out_shape=jax.ShapeDtypeStruct((T, D), BF),
-        grid=(Q, T // tm),
-        in_specs=[pl.BlockSpec((1, tm, C), lambda q, i: (0, i, q)), pl.BlockSpec((1, tm, C), lambda q, i: (1, i, q))]
-        + weight_specs()
-        + [last, last],
-        out_specs=last,
-        scratch_shapes=[pltpu.VMEM((D, C), BF)] * 2 + [pltpu.VMEM((T, D), F32)] * 2,
-        compiler_params=params(2),
+        grid=(T // tm,),
+        in_specs=[
+            pl.BlockSpec((1, tm, FF), lambda i: (0, i, 0)),
+            pl.BlockSpec((1, tm, FF), lambda i: (1, i, 0)),
+            pl.BlockSpec((S, 256, C), lambda i: (0, 0, 0), pipeline_mode=pl.Buffered(1)),
+            pl.BlockSpec((1024, C), lambda i: (0, 0), pipeline_mode=pl.Buffered(1)),
+            row,
+            row,
+        ],
+        out_specs=row,
+        scratch_shapes=[pltpu.VMEM((D, FF), BF)] * 2,
+        compiler_params=params(1),
         cost_estimate=cost(4 * T * D * FF, 75e6),
         name="dstate",
-    )(dgu, dgu, packed, packed, rest, rest, h, dy)
+    )(dgu, dgu, packed, rest, h, dy)
 
 
 def d_down_kernel(act_ref, dy_ref, out_ref):
     out_ref[...] = dot_general(act_ref[...], dy_ref[...], FIRST).astype(BF).reshape(8, 144, D)
 
 
-def d_down(act, dy, alone):
+def d_down(act, dy):
     return pl.pallas_call(
         d_down_kernel,
-        out_shape=jax.ShapeDtypeStruct((S, 144 if alone else ROWS, D), BF),
+        out_shape=jax.ShapeDtypeStruct((S, 144, D), BF),
         grid=(Q,),
         in_specs=[pl.BlockSpec((T, C), lambda q: (0, q)), pl.BlockSpec((T, D), lambda q: (0, 0))],
-        out_specs=pl.BlockSpec((8, 144, D), lambda q: (q, 0 if alone else 2, 0)),
+        out_specs=pl.BlockSpec((8, 144, D), lambda q: (q, 0, 0)),
         compiler_params=params(1),
         cost_estimate=cost(2 * T * D * FF, 35e6),
         name="d_down",
     )(act, dy)
 
 
-def d_gate_up_kernel(at_ref, dgu_ref, order_ref, *refs):
-    out_ref, rest = refs[-2:]
+def d_gate_up_kernel(at_ref, dgu_ref, order_ref, out_ref, rest):
     g = pl.program_id(0)
 
     @pl.when(g < 2 * Q)
@@ -219,28 +216,26 @@
         out_ref[...] = dot(order_ref[...], rest[...]).astype(BF).reshape(S, 32, C)
 
 
-def d_gate_up(at, dgu, order, packed=None):
+def d_gate_up(at, dgu, order):
     def block(g):
         g = jnp.minimum(g, 2 * Q - 1)
         return (g // Q, 0, g % Q)
 
     return pl.pallas_call(
         d_gate_up_kernel,
-        out_shape=jax.ShapeDtypeStruct((S, 288 if packed is None else ROWS, D), BF),
+        out_shape=jax.ShapeDtypeStruct((S, 288, D), BF),
         grid=(2 * Q + 1,),
         in_specs=[
             pl.BlockSpec((D, T), lambda g: (0, 0)),
             pl.BlockSpec((1, T, C), block),
             pl.BlockSpec((1024, 1024), lambda g: (0, 0)),
-        ]
-        + [pl.BlockSpec(memory_space=pl.ANY)] * (packed is not None),
+        ],
         out_specs=pl.BlockSpec((S, 32, C), lambda g: (0, g, 0)),
         scratch_shapes=[pltpu.VMEM((1024, C), BF)],
-        input_output_aliases={} if packed is None else {3: 0},
         compiler_params=params(1),
         cost_estimate=cost(4 * T * D * FF, 65e6),
         name="d_gate_up",
-    )(at, dgu, order, *([] if packed is None else [packed]))
+    )(at, dgu, order)
 
 
 def total_kernel(part_ref, out_ref, mine, slots, send, recv):
@@ -337,11 +332,23 @@
     return (w - 0.02 * step).astype(BF), m, v
 
 
+def across_kernel(a_ref, b_ref, c_ref, d_ref, out_ref):
+    out_ref[...] = (a_ref[...].astype(F32) + b_ref[...].astype(F32) + c_ref[...].astype(F32) + d_ref[...].astype(F32)).astype(BF)
+
+
 def across(block, n=4):
-    total = block.astype(F32)
-    for shift in range(1, n):
-        total = total + lax.ppermute(block, "r", [(i, (i + shift) % n) for i in range(n)]).astype(F32)
-    return total.astype(BF)
+    others = [lax.ppermute(block, "r", [(i, (i + shift) % n) for i in range(n)]) for shift in range(1, n)]
+    spec = pl.BlockSpec((144, C), lambda i: (i, 0))
+    return pl.pallas_call(
+        across_kernel,
+        out_shape=jax.ShapeDtypeStruct(block.shape, BF),
+        grid=(block.shape[0] // 144,),
+        in_specs=[spec] * n,
+        out_specs=spec,
+        compiler_params=params(1),
+        cost_estimate=cost(block.size * 4, block.size * 10),
+        name="across",
+    )(block, *others)
 
 
 def scattered(term):
@@ -364,26 +371,26 @@
 
         x, dy = moved(x[0], order), moved(dy[0], order)
         a0 = normed_wide(x.astype(F32)).astype(BF)
-        at0 = a0.T
+        at0, packed[0] = lax.optimization_barrier((a0.T, packed[0]))
         rest = [rest_of(packed[0], rests)]
         act0 = gate_up(a0, packed[0], rest[0])
         h1, a1 = down(act0, packed[0], x)
-        a1, packed[1] = lax.optimization_barrier((a1, packed[1]))
+        a1, at1, packed[1] = lax.optimization_barrier((a1, a1.T, packed[1]))
         rest.append(rest_of(packed[1], rests))
-        at1 = a1.T
         act1, dgu1 = back(a1, dy, packed[1], rest[1], True)
-        term1 = d_gate_up(at1, dgu1, rests, d_down(act1, dy, False))
-        term1, dgu1 = lax.optimization_barrier((term1, dgu1))
+        sum_down1 = scattered(d_down(act1, dy))
+        term1 = d_gate_up(at1, dgu1, rests)
         sum1 = scattered(term1)
         dh1 = dstate(dgu1, packed[1], rest[1], h1, dy)
-        down0, dh1 = lax.optimization_barrier((d_down(act0, dh1, True), dh1))
-        sum_down0 = scattered(down0)
+        sum_down0 = scattered(d_down(act0, dh1))
         _, dgu0 = back(a0, dh1, packed[0], rest[0], False)
-        sum0 = scattered(d_gate_up(at0, dgu0, rests))
-
-        blocks = [across(b) for b in (sum0, sum_down0, sum1)]
-        squares = summed_over_group(sum(jnp.sum(jnp.square(b.astype(F32))) for b in blocks))
-        blocks = [jnp.concatenate(blocks[:2]), blocks[2]]
+        term0 = d_gate_up(at0, dgu0, rests)
+        sum0 = scattered(term0)
+
+        early = across(jnp.concatenate([sum1, sum_down1, sum_down0]))
+        late = across(sum0)
+        squares = summed_over_group(sum(jnp.sum(jnp.square(b.astype(F32))) for b in (early, late)))
+        blocks = [jnp.concatenate([late, early[432:]]), early[:432]]
         factor = jnp.minimum(1.0, 0.5 * lax.rsqrt(squares / (2 * 3 * D * FF) + 1e-30))
         pieces = [unpack(b, order) for b in blocks]
         new = [
@@ -393,10 +400,11 @@
         return tuple(one[which] for which in range(3) for one in new)
 
     states, cut = P(("rep", "r", "s"), None, None), P(None, "s", None)
-    return jax.shard_map(
+    step = jax.shard_map(
         step,
         mesh=mesh,
         in_specs=(states, states) + (cut,) * 9,
         out_specs=(P("rep", "s", None),) * 9,
         check_vma=False,
     )
+    return step

time: 1100 us -> 1140 us (1.036)
  waiting for transfers between devices: 393 us -> 441 us
    reduce_scatter x2 -> x4, waiting for transfers between devices: 123 us -> 326 us  [scattered(): lax.psum_scatter(term.reshape(-1, C), 's', scatter_dimension=0, tiled=True)]
    unnamed x6, waiting for transfers between devices: 125 us -> 0.1 us
    ppermute x9 -> x6, waiting for transfers between devices: 69 us -> 47.5 us  [across(): lax.ppermute(block, 'r', [(i, (i + shift) % n) for i in range(n)])]
    pallas_call x5 -> x7, Pallas kernels: 256 us -> 252 us  [the longest x2 119 us: d_gate_up(): pl.pallas_call(d_gate_up_kernel, out_shape=jax.ShapeDtypeStruct((S, 288,...]
  transfers between devices with their start and end apart: 14 -> 12, of which waited for: 8 -> 8; matrix products, arithmetic and copies ran while one was open for 6% -> 6% of each run, Pallas kernels for 23% -> 19%
where the time goes in v2:
time: 1140 us; the launch traced here: 1130 us
  Pallas kernels  549 us (48%)
  waiting for transfers between devices  441 us (39%)
  local copies, waits for them, and re-layouts  55.2 us (5%)
  matrix products  33.1 us (3%)
  other arithmetic  22.5 us (2%)
  between operations  17.2 us (2%)
  starting transfers between devices  12 us (1%)
    reduce_scatter x4, waiting for transfers between devices, scattered(): lax.psum_scatter(term.reshape(-1, C), 's', scatter_dimension=0, tiled=True)  326 us
    pallas_call x2, Pallas kernels, back(): pl.pallas_call(functools.partial(back_kernel, with_act), out_shape=tuple(...  189 us
    pallas_call x2, Pallas kernels, d_gate_up(): pl.pallas_call(d_gate_up_kernel, out_shape=jax.ShapeDtypeStruct((S, 288,...  119 us
    all_gather x2, waiting for transfers between devices, step(): lax.all_gather(pack(*(w[n] for w in weights), order), 's', axis=0, tiled=...  67.3 us
    pallas_call x1, Pallas kernels, dstate(): pl.pallas_call(dstate_kernel, out_shape=jax.ShapeDtypeStruct((T, D), BF),...  64.2 us
    pallas_call x1, Pallas kernels, gate_up(): pl.pallas_call(gate_up_kernel, out_shape=jax.ShapeDtypeStruct((T, FF), BF...  62.7 us
    pallas_call x2, Pallas kernels, d_down(): pl.pallas_call(d_down_kernel, out_shape=jax.ShapeDtypeStruct((S, 144, D),...  61.8 us
    ppermute x6, waiting for transfers between devices, across(): lax.ppermute(block, 'r', [(i, (i + shift) % n) for i in range(n)])  47.5 us
  transfers between devices with their start and end apart: 12, of which 8 were waited for; matrix products, arithmetic and copies ran while one was open for 6% of the time, Pallas kernels for 19%

profile of v2, /device:TPU:0, one launch (start us, length us, event | category | flops | bytes accessed | tf_op | source)
XLA Modules:
  0.0 1129.9 jit_solution(1425293481837390840)
XLA Ops:
  21.9 8.3 fusion
  35.9 6.8 copy.51.a_ref
  42.7 6.7 copy.44.x_ref
  51.2 6.4 multiply_convert_fusion.at_ref
  57.6 8.7 fusion.2.dy_ref
  66.2 64.5 %all-gather.3.cloned.1.call-done = bf16[13824,1152]{1,0:T(8,128)(2,1)} async-done(((bf16[432,1152]{1,0:T(8,128)(2,1)}), bf16[13824,1152]{1,0:T(8,128)(2,1)}) %all-gather.3.cloned.1.call-update) | async-done | bytes 31850512 | tf_op jit(solution)/shard_map/all_gather | solution.py:368
  137.1 62.7 %gate_up.1.act_ref = bf16[2048,4608]{1,0:T(8,128)(2,1)} custom-call(bf16[2048,1152]{1,0:T(8,128)(2,1)} %copy.51.a_ref, bf16[32,432,1152]{2,1,0:T(8,128)(2,1)} %bitcast.120, bf16[32,432,1152]{2,1,0:T(8,128)(2,1)} %bitcast.121, bf16[1024,1152]{1,0:T(8,128)(2,1)} %fusion.13.gr_ref.ur_ref, bf16[1024,1152]{1,0:T(8,128)(2,1)} %fusion.13.gr_ref.ur_ref), custom_call_target="tpu_custom_call" | custom-call | flops 43486543872 | bytes 60000000 | tf_op jit(solution)/shard_map/gate_up/pallas_call | solution.py:69
  199.7 33.2 %down.1 = (bf16[2048,1152]{1,0:T(8,128)(2,1)}, bf16[2048,1152]{1,0:T(8,128)(2,1)}) custom-call(bf16[2048,4608]{1,0:T(8,128)(2,1)} %gate_up.1.act_ref, bf16[32,432,1152]{2,1,0:T(8,128)(2,1)} %bitcast.122, bf16[2048,1152]{1,0:T(8,128)(2,1)} %copy.44.x_ref), custom_call_target="tpu_custom_call" | custom-call | flops 21743271936 | bytes 45000000 | tf_op jit(solution)/shard_map/down/pallas_call | solution.py:91
  232.9 6.7 copy.45
  244.2 4.5 fusion.14.gr_ref.ur_ref.r_ref
  248.7 95.3 %back.2 = (bf16[2048,4608]{1,0:T(8,128)(2,1)}, bf16[2,2048,4608]{2,1,0:T(8,128)(2,1)}) custom-call(bf16[2048,1152]{1,0:T(8,128)(2,1)} %get-tuple-element.21.a_ref, bf16[2048,1152]{1,0:T(8,128)(2,1)} %fusion.2.dy_ref, bf16[32,432,1152]{2,1,0:T(8,128)(2,1)} %bitcast.127, bf16[32,432,1152]{2,1,0:T(8,128)(2,1)} %bitcast.128, ...), custom_call_target="tpu_custom_call" | custom-call | flops 65229815808 | bytes 130000000 | tf_op jit(solution)/shard_map/back/pallas_call | solution.py:134
  344.0 64.2 %dstate.1.dy_ref = bf16[2048,1152]{1,0:T(8,128)(2,1)} custom-call(bf16[2,2048,4608]{2,1,0:T(8,128)(2,1)} %get-tuple-element.23.dg_ref.du_ref.dgu_ref, bf16[2,2048,4608]{2,1,0:T(8,128)(2,1)} %get-tuple-element.23.dg_ref.du_ref.dgu_ref, bf16[32,432,1152]{2,1,0:T(8,128)(2,1)} %bitcast.130, bf16[1024,1152]{1,0:T(8,128)(2,1)} %fusion.14.gr_ref.ur_ref.r_ref, ...), custom_call_target="tpu_custom_call" | custom-call | flops 43486543872 | bytes 75000000 | tf_op jit(solution)/shard_map/dstate/pallas_call | solution.py:168
  408.2 94.0 %back.3.dgu_ref = bf16[2,2048,4608]{2,1,0:T(8,128)(2,1)} custom-call(bf16[2048,1152]{1,0:T(8,128)(2,1)} %copy.51.a_ref, bf16[2048,1152]{1,0:T(8,128)(2,1)} %dstate.1.dy_ref, bf16[32,432,1152]{2,1,0:T(8,128)(2,1)} %bitcast.123, bf16[32,432,1152]{2,1,0:T(8,128)(2,1)} %bitcast.124, bf16[1024,1152]{1,0:T(8,128)(2,1)} %fusion.13.gr_ref.ur_ref, ...), custom_call_target="tpu_custom_call" | custom-call | flops 65229815808 | bytes 130000000 | tf_op jit(solution)/shard_map/back/pallas_call | solution.py:134
  502.1 59.5 %d_gate_up.2 = bf16[32,288,1152]{2,1,0:T(8,128)(2,1)} custom-call(bf16[1152,2048]{1,0:T(8,128)(2,1)} %multiply_convert_fusion.at_ref, bf16[2,2048,4608]{2,1,0:T(8,128)(2,1)} %back.3.dgu_ref, bf16[1024,1024]{1,0:T(8,128)(2,1)} %fusion.10.order_ref), custom_call_target="tpu_custom_call" | custom-call | flops 43486543872 | bytes 65000000 | tf_op jit(solution)/shard_map/d_gate_up/pallas_call | solution.py:224
  561.7 59.7 %d_gate_up.3 = bf16[32,288,1152]{2,1,0:T(8,128)(2,1)} custom-call(bf16[1152,2048]{1,0:T(8,128)(2,1)} %bitcast.100, bf16[2,2048,4608]{2,1,0:T(8,128)(2,1)} %get-tuple-element.23.dg_ref.du_ref.dgu_ref, bf16[1024,1024]{1,0:T(8,128)(2,1)} %fusion.10.order_ref), custom_call_target="tpu_custom_call" | custom-call | flops 43486543872 | bytes 65000000 | tf_op jit(solution)/shard_map/d_gate_up/pallas_call | solution.py:224
  621.4 30.6 %d_down.2 = bf16[32,144,1152]{2,1,0:T(8,128)(2,1)} custom-call(bf16[2048,4608]{1,0:T(8,128)(2,1)} %get-tuple-element.26.act_ref, bf16[2048,1152]{1,0:T(8,128)(2,1)} %fusion.2.dy_ref), custom_call_target="tpu_custom_call" | custom-call | flops 21743271936 | bytes 35000000 | tf_op jit(solution)/shard_map/d_down/pallas_call | solution.py:193
  652.2 31.1 %d_down.3 = bf16[32,144,1152]{2,1,0:T(8,128)(2,1)} custom-call(bf16[2048,4608]{1,0:T(8,128)(2,1)} %gate_up.1.act_ref, bf16[2048,1152]{1,0:T(8,128)(2,1)} %dstate.1.dy_ref), custom_call_target="tpu_custom_call" | custom-call | flops 21743271936 | bytes 35000000 | tf_op jit(solution)/shard_map/d_down/pallas_call | solution.py:193
  683.3 7.1 reduce-scatter.5.cloned.1.call-done.a_ref
  696.0 126.7 %reduce-scatter.7.cloned.1.call-done = bf16[288,1152]{1,0:T(8,128)(2,1)} async-done(((bf16[9216,1152]{1,0:T(8,128)(2,1)}), bf16[288,1152]{1,0:T(8,128)(2,1)}) %reduce-scatter.7.cloned.1.call-update) | async-done | bytes 663568 | tf_op jit(solution)/shard_map/reduce_scatter | solution.py:355
  823.9 95.9 %reduce-scatter.9.cloned.1.call-done = bf16[144,1152]{1,0:T(8,128)(2,1)} async-done(((bf16[4608,1152]{1,0:T(8,128)(2,1)}), bf16[144,1152]{1,0:T(8,128)(2,1)}) %reduce-scatter.9.cloned.1.call-update) | async-done | bytes 331792 | tf_op jit(solution)/shard_map/reduce_scatter | solution.py:355
  920.9 96.1 %reduce-scatter.11.cloned.1.call-done = bf16[144,1152]{1,0:T(8,128)(2,1)} async-done(((bf16[4608,1152]{1,0:T(8,128)(2,1)}), bf16[144,1152]{1,0:T(8,128)(2,1)}) %reduce-scatter.11.cloned.1.call-update) | async-done | bytes 331792 | tf_op jit(solution)/shard_map/reduce_scatter | solution.py:355
  1030.3 20.1 %collective-permute-done.3.b_ref = bf16[576,1152]{1,0:T(8,128)(2,1)} collective-permute-done((bf16[576,1152]{1,0:T(8,128)(2,1)S(1)}, bf16[576,1152]{1,0:T(8,128)(2,1)}, u32[]{:S(2)}, u32[]{:S(2)}) %collective-permute-start.3) | collective-permute-done | bytes 1327136 | tf_op jit(solution)/shard_map/ppermute | solution.py:340
  1050.4 27.4 %collective-permute-done.4.c_ref = bf16[576,1152]{1,0:T(8,128)(2,1)} collective-permute-done((bf16[576,1152]{1,0:T(8,128)(2,1)S(1)}, bf16[576,1152]{1,0:T(8,128)(2,1)}, u32[]{:S(2)}, u32[]{:S(2)}) %collective-permute-start.4) | collective-permute-done | bytes 1327136 | tf_op jit(solution)/shard_map/ppermute | solution.py:340
  1091.8 11.8 %total.1 = f32[8,128]{1,0:T(8,128)} custom-call(f32[8,128]{1,0:T(8,128)} %fusion.95.part_ref), custom_call_target="tpu_custom_call" | custom-call | tf_op jit(solution)/shard_map/total/pallas_call | solution.py:278
  (143 shorter events, 84.8 us)
Async XLA Ops:
  7.2 5.4 copy-start.3
  7.2 123.6 %all-gather.3.cloned.1.call-start = ((), (), s32[]{:S(2)}) async-start(), calls=%async_computation.4 | async-start | bytes 32845824 | tf_op jit(solution)/shard_map/all_gather | solution.py:368
  7.2 50.3 %copy-start.17 = (s32[1152]{0:T(1024)}, s32[1152]{0:T(1024)S(1)}, u32[]{:S(2)}) copy-start(s32[1152]{0:T(1024)S(1)} %fusion.74) | copy-start | bytes 13828
  18.7 223.6 %all-gather.5.cloned.1.call-start = ((), (), s32[]{:S(2)}) async-start(), calls=%async_computation.5 | async-start | bytes 32845824 | tf_op jit(solution)/shard_map/all_gather | solution.py:368
  21.4 669.0 %reduce-scatter.5.cloned.1.call-start = ((), (), s32[]{:S(2)}) async-start(), calls=%async_computation.6 | async-start | bytes 21897216 | tf_op jit(solution)/shard_map/reduce_scatter | solution.py:355
  49.4 8.1 slice-start
  51.2 6.4 slice-start.1
  561.6 261.1 %reduce-scatter.7.cloned.1.call-start = ((), (), s32[]{:S(2)}) async-start(), calls=%async_computation.7 | async-start | bytes 21897216 | tf_op jit(solution)/shard_map/reduce_scatter | solution.py:355
  621.4 298.5 %reduce-scatter.9.cloned.1.call-start = ((), (), s32[]{:S(2)}) async-start(), calls=%async_computation.8 | async-start | bytes 10948608 | tf_op jit(solution)/shard_map/reduce_scatter | solution.py:355
  652.1 364.9 %reduce-scatter.11.cloned.1.call-start = ((), (), s32[]{:S(2)}) async-start(), calls=%async_computation.9 | async-start | bytes 10948608 | tf_op jit(solution)/shard_map/reduce_scatter | solution.py:355
  690.4 331.8 %collective-permute-start = (bf16[288,1152]{1,0:T(8,128)(2,1)}, bf16[288,1152]{1,0:T(8,128)(2,1)S(1)}, u32[]{:S(2)}, u32[]{:S(2)}) collective-permute-start(bf16[288,1152]{1,0:T(8,128)(2,1)} %reduce-scatter.5.cloned.1.call-done.a_ref), channel_id=1, source_target_pairs={{0,32},{32,64},{64,96},{96,0},{1,33},{33,65},{65,97},{97,1},{2,34}... | collective-permute-start | bytes 1990664 | tf_op jit(solution)/shard_map/ppermute | solution.py:340
  691.9 331.8 %collective-permute-start.1 = (bf16[288,1152]{1,0:T(8,128)(2,1)}, bf16[288,1152]{1,0:T(8,128)(2,1)}, u32[]{:S(2)}, u32[]{:S(2)}) collective-permute-start(bf16[288,1152]{1,0:T(8,128)(2,1)} %reduce-scatter.5.cloned.1.call-done.a_ref), channel_id=1, source_target_pairs={{0,64},{32,96},{64,0},{96,32},{1,65},{33,97},{65,1},{97,33},{2,66}... | collective-permute-start | bytes 1990664 | tf_op jit(solution)/shard_map/ppermute | solution.py:340
  694.6 329.1 %collective-permute-start.2 = (bf16[288,1152]{1,0:T(8,128)(2,1)}, bf16[288,1152]{1,0:T(8,128)(2,1)}, u32[]{:S(2)}, u32[]{:S(2)}) collective-permute-start(bf16[288,1152]{1,0:T(8,128)(2,1)} %reduce-scatter.5.cloned.1.call-done.a_ref), channel_id=1, source_target_pairs={{0,96},{32,0},{64,32},{96,64},{1,97},{33,1},{65,33},{97,65},{2,98}... | collective-permute-start | bytes 1990664 | tf_op jit(solution)/shard_map/ppermute | solution.py:340
  1018.0 8.5 copy-start.6
  1018.0 32.4 %collective-permute-start.3 = (bf16[576,1152]{1,0:T(8,128)(2,1)S(1)}, bf16[576,1152]{1,0:T(8,128)(2,1)}, u32[]{:S(2)}, u32[]{:S(2)}) collective-permute-start(bf16[576,1152]{1,0:T(8,128)(2,1)S(1)} %constant_dynamic-update-slice_fusion.8.a_ref), channel_id=1, source_target_pairs={{0,32},{32,64},{64,96},{96,0},{1,33},{33,65},{65,97},{97,1},{2,34}... | collective-permute-start | bytes 3981320 | tf_op jit(solution)/shard_map/ppermute | solution.py:340
  1019.5 58.3 %collective-permute-start.4 = (bf16[576,1152]{1,0:T(8,128)(2,1)S(1)}, bf16[576,1152]{1,0:T(8,128)(2,1)}, u32[]{:S(2)}, u32[]{:S(2)}) collective-permute-start(bf16[576,1152]{1,0:T(8,128)(2,1)S(1)} %constant_dynamic-update-slice_fusion.8.a_ref), channel_id=1, source_target_pairs={{0,64},{32,96},{64,0},{96,32},{1,65},{33,97},{65,1},{97,33},{2,66}... | collective-permute-start | bytes 3981320 | tf_op jit(solution)/shard_map/ppermute | solution.py:340
  1022.2 55.6 %collective-permute-start.5 = (bf16[576,1152]{1,0:T(8,128)(2,1)S(1)}, bf16[576,1152]{1,0:T(8,128)(2,1)}, u32[]{:S(2)}, u32[]{:S(2)}) collective-permute-start(bf16[576,1152]{1,0:T(8,128)(2,1)S(1)} %constant_dynamic-update-slice_fusion.8.a_ref), channel_id=1, source_target_pairs={{0,96},{32,0},{64,32},{96,64},{1,97},{33,1},{65,33},{97,65},{2,98}... | collective-permute-start | bytes 3981320 | tf_op jit(solution)/shard_map/ppermute | solution.py:340
  1030.3 54.5 %copy-start.18 = (s32[1152]{0:T(1024)S(1)}, s32[1152]{0:T(1024)}, u32[]{:S(2)}) copy-start(s32[1152]{0:T(1024)} %copy-done.17) | copy-start | bytes 13828
  1089.7 15.9 %copy-start.2 = (bf16[2,36,4608]{2,0,1:T(2,128)(2,1)S(1)}, bf16[2,36,4608]{2,0,1:T(2,128)(2,1)}, u32[]{:S(2)}) copy-start(bf16[2,36,4608]{2,0,1:T(2,128)(2,1)} %param.13) | copy-start | bytes 1990660
  1089.8 15.9 %copy-start.4 = (bf16[2,36,4608]{2,0,1:T(2,128)(2,1)S(1)}, bf16[2,36,4608]{2,0,1:T(2,128)(2,1)}, u32[]{:S(2)}) copy-start(bf16[2,36,4608]{2,0,1:T(2,128)(2,1)} %param.14) | copy-start | bytes 1990660
  1089.8 15.9 %copy-start.9 = (bf16[1,36,4608]{2,1,0:T(8,128)(2,1)S(1)}, bf16[1,36,4608]{2,1,0:T(8,128)(2,1)}, u32[]{:S(2)}) copy-start(bf16[1,36,4608]{2,1,0:T(8,128)(2,1)} %maximum_bitcast_fusion) | copy-start | bytes 995332
  1115.7 4.8 copy-start.13
  1115.7 4.8 copy-start.15
  1115.7 4.8 copy-start.16
  (9 other events, 17.1 us)
Sparse Core Ops, SparseCore 0:
  18.9 111.8 all-gather.2
  133.7 108.6 all-gather.4
  561.8 128.5 reduce-scatter.4
  694.2 128.5 reduce-scatter.6
  826.5 93.2 reduce-scatter.8
  923.6 93.3 reduce-scatter.10
